TPU v7x, 32 devices: a whole 2x2x4 slice. The times are simulated.
32 devices in a mesh: seq: 16 (over z, y, x), dp: 2 (over core).
Axes of the slice: x: 2, y: 2, z: 4, core: 2. Of those that a mesh axis runs over, the one named last changes fastest.
Arguments:
- block_pos: int32 [2, 32], P('dp'), may hold values from 0 to 31, as said below
- queries: bfloat16 [2, 2048, 2048], P('dp', 'seq'), may hold values from -8 to 8
- keys: bfloat16 [2, 2048, 2048], P('dp', 'seq'), may hold values from -4 to 4
- values: bfloat16 [2, 2048, 2048], P('dp', 'seq'), may hold values from -4 to 4
- attn_out: bfloat16 [2, 2048, 2048], P('dp', 'seq'), may hold values from -4 to 4, as said below
- log_sums: float32 [2, 16, 2048], P('dp', None, 'seq'), as said below
- grad_out: bfloat16 [2, 2048, 2048], P('dp', 'seq'), may hold values from -0.375 to 0.375
- out_weight: bfloat16 [2048, 2048], replicated, may hold values from -12 to 12
Outputs:
- grad_queries: bfloat16 [2, 2048, 2048], P('dp', 'seq')
- grad_keys: bfloat16 [2, 2048, 2048], P('dp', 'seq')
- grad_values: bfloat16 [2, 2048, 2048], P('dp', 'seq')
- grad_weight: float32 [2048, 2048], P('seq')
Inputs may be any that keep to these rules, and one draw needn't show every extreme that they name: Each row is a permutation of 0 to 31; row block c (rows c * 64 to c * 64 + 63) holds the rows at positions block_pos[b, c] * 64 onward, in order. attn_out is the forward attention output: per head, exp(scores - log_sums) on the allowed keys times values, rounded to bfloat16. log_sums[b, h, t] is the log of the sum of exp(scores[b, h, t, u]) over the keys u with pos[b, u] <= pos[b, t].
All inputs are finite; a program needn't handle non-finite values.
Results may differ from a plain program's by a relative error of at most 0.0075.
Values may be sent and summed in bfloat16 or wider, within the bound.
A program may use at most 320 MiB of HBM per device.

v0:
```python
import jax
import jax.numpy as jnp
from jax import lax
from jax.sharding import PartitionSpec as P


def shifted(shard, axis, by):
    count = lax.axis_size(axis)
    return lax.ppermute(shard, axis, [(i, (i + by) % count) for i in range(count)])


def slot_positions(table_row, owners, half_rows):
    slot_ids = owners[:, None] * 2 + jnp.arange(2, dtype=jnp.int32)[None, :]
    pick_rows = (
        slot_ids[:, :, None] == jnp.arange(table_row.shape[0], dtype=jnp.int32)[None, None, :]
    ).astype(jnp.int32)
    block_ids = jnp.sum(pick_rows * table_row[None, None, :], axis=-1)
    offsets = jnp.arange(half_rows, dtype=jnp.int32)
    return (block_ids[:, :, None] * half_rows + offsets[None, None, :]).reshape(
        owners.shape[0], 2 * half_rows
    )


def block_core(
    query_rows, grad_rows, log_block, delta_block, key_rows, value_rows, allowed, scaling
):
    head_count = log_block.shape[0]
    query_len = query_rows.shape[0]
    key_len = key_rows.shape[0]
    query_heads = query_rows.reshape(query_len, head_count, -1)
    grad_split = grad_rows.reshape(query_len, head_count, -1)
    key_heads = key_rows.reshape(key_len, head_count, -1)
    value_heads = value_rows.reshape(key_len, head_count, -1)
    scores = (
        jnp.einsum("ahd,bhd->hab", query_heads, key_heads, preferred_element_type=jnp.float32)
        * scaling
    )
    attn_probs = jnp.where(allowed[None], jnp.exp(scores - log_block[:, :, None]), 0.0)
    probs_low = attn_probs.astype(jnp.bfloat16)
    dprobs = jnp.einsum("ahd,bhd->hab", grad_split, value_heads, preferred_element_type=jnp.float32)
    dscores = attn_probs * (dprobs - delta_block[:, :, None])
    dscores_low = dscores.astype(jnp.bfloat16)
    value_part = jnp.einsum(
        "hab,ahd->bhd", probs_low, grad_split, preferred_element_type=jnp.float32
    )
    key_part = (
        jnp.einsum("hab,ahd->bhd", dscores_low, query_heads, preferred_element_type=jnp.float32)
        * scaling
    )
    query_part = (
        jnp.einsum("hab,bhd->ahd", dscores_low, key_heads, preferred_element_type=jnp.float32)
        * scaling
    )
    return (
        query_part.reshape(query_len, -1),
        key_part.reshape(key_len, -1),
        value_part.reshape(key_len, -1),
    )


def block_grads(
    query_rows, grad_rows, log_block, delta_block, key_rows, value_rows, allowed, scaling
):
    parts = block_core(
        query_rows, grad_rows, log_block, delta_block, key_rows, value_rows, allowed, scaling
    )
    return (parts[0], parts[1].astype(jnp.bfloat16), parts[2].astype(jnp.bfloat16))


def per_device(block_pos, queries, keys, values, attn_out, log_sums, grad_out, out_weight):
    dev_count = lax.axis_size("seq")
    grid_side = 4 + 4 * (dev_count // 64)
    my_index = lax.axis_index("seq")
    table_row = block_pos[0]
    own_queries = queries[0]
    tok_rows = own_queries.shape[0]
    half_rows = tok_rows // 2
    head_count = log_sums.shape[1]
    width_all = own_queries.shape[1]
    scaling = (width_all // head_count) ** (-0.5)
    cotangent = grad_out[0]
    grad_heads = lax.dot_general(
        cotangent, out_weight, (((1,), (1,)), ((), ())), preferred_element_type=jnp.float32
    ).astype(jnp.bfloat16)
    deltas = jnp.einsum(
        "ahd,ahd->ha",
        grad_heads.reshape(tok_rows, head_count, -1),
        attn_out[0].reshape(tok_rows, head_count, -1),
        preferred_element_type=jnp.float32,
    )
    query_pack = (own_queries[None], grad_heads[None], log_sums[0][None], deltas[None])
    key_pack = (keys[0][None], values[0][None])
    query_list = [query_pack]
    key_list = [key_pack]
    for offset in range(1, grid_side):
        query_list.append(
            (
                shifted(query_pack[0].astype(jnp.float32), "seq", offset).astype(jnp.bfloat16),
                shifted(query_pack[1].astype(jnp.float32), "seq", offset).astype(jnp.bfloat16),
                shifted(query_pack[2], "seq", offset),
                shifted(query_pack[3], "seq", offset),
            )
        )
        key_list.append(shifted((key_pack[0], key_pack[1]), "seq", offset * grid_side))
    query_stack = tuple(
        (jnp.concatenate([parcel[member] for parcel in query_list], axis=0) for member in range(4))
    )
    key_stack = tuple(
        (jnp.concatenate([parcel[member] for parcel in key_list], axis=0) for member in range(2))
    )
    query_rows = query_stack[0].reshape(-1, width_all)
    grad_rows = query_stack[1].reshape(-1, width_all)
    log_block = jnp.transpose(query_stack[2], (1, 0, 2)).reshape(head_count, -1)
    delta_block = jnp.transpose(query_stack[3], (1, 0, 2)).reshape(head_count, -1)
    query_owners = (my_index - jnp.arange(grid_side, dtype=jnp.int32)) % dev_count
    key_owners = (my_index - jnp.arange(grid_side, dtype=jnp.int32) * grid_side) % dev_count
    query_pos = slot_positions(table_row, query_owners, half_rows).reshape(-1)
    key_pos = slot_positions(table_row, key_owners, half_rows)
    query_total = jnp.zeros((grid_side * tok_rows, width_all), jnp.float32)
    key_results = []
    for offset in range(grid_side):
        key_now = key_stack[0][offset]
        value_now = key_stack[1][offset]
        allowed = key_pos[offset][None, :] <= query_pos[:, None]
        results = block_grads(
            query_rows, grad_rows, log_block, delta_block, key_now, value_now, allowed, scaling
        )
        query_total = query_total + results[0]
        key_results.append((results[1], results[2]))
    query_parts = query_total.astype(jnp.bfloat16).reshape(grid_side, tok_rows, width_all)
    query_sum = query_parts[0].astype(jnp.float32)
    for offset in range(1, grid_side):
        query_sum = query_sum + shifted(query_parts[offset], "seq", -offset).astype(jnp.float32)
    key_sum = key_results[0][0].astype(jnp.float32)
    value_sum = key_results[0][1].astype(jnp.float32)
    for offset in range(1, grid_side):
        returned = shifted(
            (key_results[offset][0], key_results[offset][1]), "seq", -offset * grid_side
        )
        key_sum = key_sum + returned[0].astype(jnp.float32)
        value_sum = value_sum + returned[1].astype(jnp.float32)
    columns = attn_out[0]
    weight_share = lax.psum_scatter(
        lax.dot_general(
            columns, cotangent, (((0,), (0,)), ((), ())), preferred_element_type=jnp.float32
        ),
        ("seq", "dp"),
        scatter_dimension=0,
        tiled=True,
    )
    weight_share = lax.all_gather(
        weight_share.astype(jnp.bfloat16), "dp", axis=0, tiled=True
    ).astype(weight_share.dtype)
    return (
        query_sum.astype(jnp.bfloat16)[None],
        key_sum.astype(jnp.bfloat16)[None],
        value_sum.astype(jnp.bfloat16)[None],
        weight_share,
    )


def solution(mesh):
    in_specs = (
        P("dp", None),
        P("dp", "seq", None),
        P("dp", "seq", None),
        P("dp", "seq", None),
        P("dp", "seq", None),
        P("dp", None, "seq"),
        P("dp", "seq", None),
        P(),
    )
    out_specs = (P("dp", "seq", None), P("dp", "seq", None), P("dp", "seq", None), P("seq", None))
    return jax.shard_map(
        per_device, mesh=mesh, in_specs=in_specs, out_specs=out_specs, check_vma=False
    )
```

profile of v0, /device:TPU:3, one launch (start us, length us, event | category | flops | bytes accessed | tf_op | source)
XLA Modules:
  0.0 440.4 jit_solution(10252099439416319301)
XLA Ops:
  8.2 9.2 %fusion.55 = f32[2048,2048]{1,0:T(8,128)} fusion(bf16[1,128,2048]{2,1,0:T(8,128)(2,1)} %param.12, bf16[1,128,2048]{2,1,0:T(8,128)(2,1)S(1)} %copy-done), kind=kOutput, calls=%fused_computation.62 | convolution fusion | flops 1073741824 | bytes 17825792 | tf_op jit(solution)/shard_map/dot_general | solution.py:144
  21.9 6.3 %convolution_convert_fusion = bf16[128,2048]{1,0:T(8,128)(2,1)S(1)} fusion(bf16[2048,2048]{1,0:T(8,128)(2,1)} %param.15, bf16[1,128,2048]{2,1,0:T(8,128)(2,1)S(1)} %copy-done), kind=kOutput, calls=%fused_computation.13 | convolution fusion | flops 1074003968 | bytes 9437184 | tf_op jit(solution)/shard_map/dot_general | solution.py:82
  36.9 15.1 %collective-permute-done.10 = f32[1,16,128]{2,0,1:T(1,128)S(1)} collective-permute-done((f32[1,16,128]{2,0,1:T(1,128)S(1)}, f32[1,16,128]{2,0,1:T(1,128)S(1)}, u32[]{:S(2)}, u32[]{:S(2)}) %collective-permute-start.10) | collective-permute-done | bytes 8224 | tf_op jit(solution)/shard_map/ppermute | solution.py:9
  52.0 3.8 collective-permute-start.6
  58.3 21.9 %collective-permute-done = bf16[1,128,2048]{2,1,0:T(8,128)(2,1)S(1)} collective-permute-done((bf16[1,128,2048]{2,1,0:T(8,128)(2,1)S(1)}, bf16[1,128,2048]{2,1,0:T(8,128)(2,1)S(1)}, u32[]{:S(2)}, u32[]{:S(2)}) %collective-permute-start) | collective-permute-done | bytes 524320 | tf_op jit(solution)/shard_map/ppermute | solution.py:9
  80.2 3.9 collective-permute-start.17
  88.5 19.1 %collective-permute-done.7 = bf16[1,128,2048]{2,1,0:T(8,128)(2,1)} collective-permute-done((bf16[1,128,2048]{2,1,0:T(8,128)(2,1)S(1)}, bf16[1,128,2048]{2,1,0:T(8,128)(2,1)}, u32[]{:S(2)}, u32[]{:S(2)}) %collective-permute-start.7) | collective-permute-done | bytes 524320 | tf_op jit(solution)/shard_map/ppermute | solution.py:9
  107.6 3.6 collective-permute-done.6
  111.2 6.3 %collective-permute-start.16 = (bf16[1,128,2048]{1,2,0:T(8,128)(2,1)S(1)}, bf16[1,128,2048]{1,2,0:T(8,128)(2,1)}, u32[]{:S(2)}, u32[]{:S(2)}) collective-permute-start(bf16[1,128,2048]{1,2,0:T(8,128)(2,1)S(1)} %copy.160), channel_id=1, source_target_pairs={{0,24},{2,26},{4,28},{6,30},{8,0},{10,2},{12,4},{14,6},{16,8},{18,... | collective-permute-start | bytes 1572872 | tf_op jit(solution)/shard_map/ppermute | solution.py:9
  121.1 4.3 copy.133
  130.4 8.1 %collective-permute-done.14 = bf16[1,128,2048]{1,2,0:T(8,128)(2,1)} collective-permute-done((bf16[1,128,2048]{1,2,0:T(8,128)(2,1)S(1)}, bf16[1,128,2048]{1,2,0:T(8,128)(2,1)}, u32[]{:S(2)}, u32[]{:S(2)}) %collective-permute-start.14) | collective-permute-done | bytes 524320 | tf_op jit(solution)/shard_map/ppermute | solution.py:9
  140.4 20.6 %collective-permute-done.15 = bf16[1,128,2048]{1,2,0:T(8,128)(2,1)} collective-permute-done((bf16[1,128,2048]{1,2,0:T(8,128)(2,1)}, bf16[1,128,2048]{1,2,0:T(8,128)(2,1)}, u32[]{:S(2)}, u32[]{:S(2)}) %collective-permute-start.15) | collective-permute-done | bytes 524320 | tf_op jit(solution)/shard_map/ppermute | solution.py:9
  161.0 4.3 multiply_convert_fusion.2
  171.4 4.9 %multiply_convert_fusion.3 = bf16[16,512,128]{2,1,0:T(8,128)(2,1)S(1)} fusion(f32[16,512,128]{2,1,0:T(8,128)S(1)} %fusion.76, bf16[512,16,128]{0,2,1:T(8,128)(2,1)S(1)} %copy-done.18, bf16[128,16,128]{0,2,1:T(8,128)(2,1)} %bitcast.9, f32[16,512]{1,0:T(8,128)S(1)} %bitcast.158, f32[16,512]{1,0:T(8,128)S(1)} %copy_bitcast_fusion.1, ...), kind=kOutput, calls=%fused_computation.5 | convolution fusion | flops 274726912 | bytes 9043968 | tf_op jit(solution)/shard_map/ahd,bhd->hab/dot_general | solution.py:40
  176.3 3.2 multiply_convert_fusion.4
  180.9 4.4 multiply_convert_fusion.1
  193.4 60.6 %collective-permute-start.19 = (bf16[128,2048]{0,1:T(8,128)(2,1)}, bf16[128,2048]{0,1:T(8,128)(2,1)}, u32[]{:S(2)}, u32[]{:S(2)}) collective-permute-start(bf16[128,2048]{0,1:T(8,128)(2,1)} %bitcast.17), channel_id=1, source_target_pairs={{0,28},{2,30},{4,0},{6,2},{8,4},{10,6},{12,8},{14,10},{16,12},{18,... | collective-permute-start | bytes 1572872 | tf_op jit(solution)/shard_map/ppermute | solution.py:9
  254.0 49.8 %collective-permute-start.18 = (bf16[128,2048]{0,1:T(8,128)(2,1)}, bf16[128,2048]{0,1:T(8,128)(2,1)}, u32[]{:S(2)}, u32[]{:S(2)}) collective-permute-start(bf16[128,2048]{0,1:T(8,128)(2,1)} %bitcast.151), channel_id=1, source_target_pairs={{0,30},{2,0},{4,2},{6,4},{8,6},{10,8},{12,10},{14,12},{16,14},{18,... | collective-permute-start | bytes 1572872 | tf_op jit(solution)/shard_map/ppermute | solution.py:9
  303.8 3.1 fusion.32
  330.8 5.2 %fusion.36 = f32[16,128,128]{2,1,0:T(8,128)} fusion(bf16[512,16,128]{0,2,1:T(8,128)(2,1)} %copy.133, f32[16,512,128]{2,1,0:T(8,128)} %copy-done.10, f32[16,512]{1,0:T(8,128)S(1)} %copy_bitcast_fusion.1, pred[512,128]{1,0:T(8,128)(4,1)S(1)} %get-tuple-element.25), kind=kOutput, calls=%fused_computation.46 | convolution fusion | flops 273154048 | bytes 7438336 | tf_op jit(solution)/shard_map/hab,ahd->bhd/dot_general | solution.py:43
  342.6 37.8 %collective-permute-start.25 = (bf16[128,2048]{1,0:T(8,128)(2,1)}, bf16[128,2048]{1,0:T(8,128)(2,1)}, u32[]{:S(2)}, u32[]{:S(2)}) collective-permute-start(bf16[128,2048]{1,0:T(8,128)(2,1)} %copy.138), channel_id=1, source_target_pairs={{0,16},{2,18},{4,20},{6,22},{8,24},{10,26},{12,28},{14,30},{16,0},... | collective-permute-start | bytes 1572872 | tf_op jit(solution)/shard_map/ppermute | solution.py:9
  384.5 7.9 %collective-permute-done.22 = bf16[128,2048]{1,0:T(8,128)(2,1)} collective-permute-done((bf16[128,2048]{1,0:T(8,128)(2,1)}, bf16[128,2048]{1,0:T(8,128)(2,1)}, u32[]{:S(2)}, u32[]{:S(2)}) %collective-permute-start.22) | collective-permute-done | bytes 524320 | tf_op jit(solution)/shard_map/ppermute | solution.py:9
  392.4 23.3 %collective-permute-done.21 = bf16[128,2048]{1,0:T(8,128)(2,1)} collective-permute-done((bf16[128,2048]{1,0:T(8,128)(2,1)}, bf16[128,2048]{1,0:T(8,128)(2,1)}, u32[]{:S(2)}, u32[]{:S(2)}) %collective-permute-start.21) | collective-permute-done | bytes 524320 | tf_op jit(solution)/shard_map/ppermute | solution.py:9
  418.1 8.7 %collective-permute-done.24 = bf16[128,2048]{1,0:T(8,128)(2,1)S(1)} collective-permute-done((bf16[128,2048]{1,0:T(8,128)(2,1)}, bf16[128,2048]{1,0:T(8,128)(2,1)S(1)}, u32[]{:S(2)}, u32[]{:S(2)}) %collective-permute-start.24) | collective-permute-done | bytes 524320 | tf_op jit(solution)/shard_map/ppermute | solution.py:9
  (166 shorter events, 90.4 us)
Async XLA Ops:
  7.2 421.9 %reduce-scatter.2.cloned.1.call-start = ((), (), s32[]{:S(2)}) async-start(), calls=%async_computation.1 | async-start | bytes 17301504 | tf_op jit(solution)/shard_map/reduce_scatter | solution.py:143
  31.4 20.6 %collective-permute-start.1 = (bf16[1,128,2048]{2,1,0:T(8,128)(2,1)S(1)}, bf16[1,128,2048]{2,1,0:T(8,128)(2,1)S(1)}, u32[]{:S(2)}, u32[]{:S(2)}) collective-permute-start(bf16[1,128,2048]{2,1,0:T(8,128)(2,1)S(1)} %copy-done.24), channel_id=1, source_target_pairs={{0,4},{2,6},{4,8},{6,10},{8,12},{10,14},{12,16},{14,18},{16,20},{1... | collective-permute-start | bytes 1572872 | tf_op jit(solution)/shard_map/ppermute | solution.py:9
  33.2 18.8 %collective-permute-start.10 = (f32[1,16,128]{2,0,1:T(1,128)S(1)}, f32[1,16,128]{2,0,1:T(1,128)S(1)}, u32[]{:S(2)}, u32[]{:S(2)}) collective-permute-start(f32[1,16,128]{2,0,1:T(1,128)S(1)} %bitcast.162), channel_id=1, source_target_pairs={{0,4},{2,6},{4,8},{6,10},{8,12},{10,14},{12,16},{14,18},{16,20},{1... | collective-permute-start | bytes 24584 | tf_op jit(solution)/shard_map/ppermute | solution.py:9
  34.5 17.5 %collective-permute-start.9 = (f32[1,16,128]{2,0,1:T(1,128)S(1)}, f32[1,16,128]{2,0,1:T(1,128)S(1)}, u32[]{:S(2)}, u32[]{:S(2)}) collective-permute-start(f32[1,16,128]{2,0,1:T(1,128)S(1)} %bitcast.163), channel_id=1, source_target_pairs={{0,2},{2,4},{4,6},{6,8},{8,10},{10,12},{12,14},{14,16},{16,18},{18... | collective-permute-start | bytes 24584 | tf_op jit(solution)/shard_map/ppermute | solution.py:9
  35.3 44.9 %collective-permute-start = (bf16[1,128,2048]{2,1,0:T(8,128)(2,1)S(1)}, bf16[1,128,2048]{2,1,0:T(8,128)(2,1)S(1)}, u32[]{:S(2)}, u32[]{:S(2)}) collective-permute-start(bf16[1,128,2048]{2,1,0:T(8,128)(2,1)S(1)} %copy-done.24), channel_id=1, source_target_pairs={{0,2},{2,4},{4,6},{6,8},{8,10},{10,12},{12,14},{14,16},{16,18},{18... | collective-permute-start | bytes 1572872 | tf_op jit(solution)/shard_map/ppermute | solution.py:9
  35.7 48.5 %collective-permute-start.2 = (bf16[1,128,2048]{2,1,0:T(8,128)(2,1)S(1)}, bf16[1,128,2048]{2,1,0:T(8,128)(2,1)}, u32[]{:S(2)}, u32[]{:S(2)}) collective-permute-start(bf16[1,128,2048]{2,1,0:T(8,128)(2,1)S(1)} %copy-done.24), channel_id=1, source_target_pairs={{0,6},{2,8},{4,10},{6,12},{8,14},{10,16},{12,18},{14,20},{16,22},{... | collective-permute-start | bytes 1572872 | tf_op jit(solution)/shard_map/ppermute | solution.py:9
  52.0 34.0 %collective-permute-start.8 = (bf16[1,128,2048]{2,1,0:T(8,128)(2,1)S(1)}, bf16[1,128,2048]{2,1,0:T(8,128)(2,1)}, u32[]{:S(2)}, u32[]{:S(2)}) collective-permute-start(bf16[1,128,2048]{2,1,0:T(8,128)(2,1)S(1)} %bitcast.132), channel_id=1, source_target_pairs={{0,6},{2,8},{4,10},{6,12},{8,14},{10,16},{12,18},{14,20},{16,22},{... | collective-permute-start | bytes 1572872 | tf_op jit(solution)/shard_map/ppermute | solution.py:9
  52.0 55.6 %collective-permute-start.7 = (bf16[1,128,2048]{2,1,0:T(8,128)(2,1)S(1)}, bf16[1,128,2048]{2,1,0:T(8,128)(2,1)}, u32[]{:S(2)}, u32[]{:S(2)}) collective-permute-start(bf16[1,128,2048]{2,1,0:T(8,128)(2,1)S(1)} %bitcast.133), channel_id=1, source_target_pairs={{0,4},{2,6},{4,8},{6,10},{8,12},{10,14},{12,16},{14,18},{16,20},{1... | collective-permute-start | bytes 1572872 | tf_op jit(solution)/shard_map/ppermute | solution.py:9
  52.0 59.2 %collective-permute-start.6 = (bf16[1,128,2048]{2,1,0:T(8,128)(2,1)S(1)}, bf16[1,128,2048]{2,1,0:T(8,128)(2,1)}, u32[]{:S(2)}, u32[]{:S(2)}) collective-permute-start(bf16[1,128,2048]{2,1,0:T(8,128)(2,1)S(1)} %bitcast.134), channel_id=1, source_target_pairs={{0,2},{2,4},{4,6},{6,8},{8,10},{10,12},{12,14},{14,16},{16,18},{18... | collective-permute-start | bytes 1572872 | tf_op jit(solution)/shard_map/ppermute | solution.py:9
  80.2 100.7 %collective-permute-start.17 = (bf16[1,128,2048]{1,2,0:T(8,128)(2,1)}, bf16[1,128,2048]{1,2,0:T(8,128)(2,1)}, u32[]{:S(2)}, u32[]{:S(2)}) collective-permute-start(bf16[1,128,2048]{1,2,0:T(8,128)(2,1)} %copy.102), channel_id=1, source_target_pairs={{0,24},{2,26},{4,28},{6,30},{8,0},{10,2},{12,4},{14,6},{16,8},{18,... | collective-permute-start | bytes 1572872 | tf_op jit(solution)/shard_map/ppermute | solution.py:9
  84.2 54.3 %collective-permute-start.14 = (bf16[1,128,2048]{1,2,0:T(8,128)(2,1)S(1)}, bf16[1,128,2048]{1,2,0:T(8,128)(2,1)}, u32[]{:S(2)}, u32[]{:S(2)}) collective-permute-start(bf16[1,128,2048]{1,2,0:T(8,128)(2,1)S(1)} %copy.160), channel_id=1, source_target_pairs={{0,16},{2,18},{4,20},{6,22},{8,24},{10,26},{12,28},{14,30},{16,0},... | collective-permute-start | bytes 1572872 | tf_op jit(solution)/shard_map/ppermute | solution.py:9
  86.0 75.0 %collective-permute-start.15 = (bf16[1,128,2048]{1,2,0:T(8,128)(2,1)}, bf16[1,128,2048]{1,2,0:T(8,128)(2,1)}, u32[]{:S(2)}, u32[]{:S(2)}) collective-permute-start(bf16[1,128,2048]{1,2,0:T(8,128)(2,1)} %copy.102), channel_id=1, source_target_pairs={{0,16},{2,18},{4,20},{6,22},{8,24},{10,26},{12,28},{14,30},{16,0},... | collective-permute-start | bytes 1572872 | tf_op jit(solution)/shard_map/ppermute | solution.py:9
  107.6 63.8 %collective-permute-start.13 = (bf16[1,128,2048]{1,2,0:T(8,128)(2,1)}, bf16[1,128,2048]{1,2,0:T(8,128)(2,1)}, u32[]{:S(2)}, u32[]{:S(2)}) collective-permute-start(bf16[1,128,2048]{1,2,0:T(8,128)(2,1)} %copy.102), channel_id=1, source_target_pairs={{0,8},{2,10},{4,12},{6,14},{8,16},{10,18},{12,20},{14,22},{16,24},... | collective-permute-start | bytes 1572872 | tf_op jit(solution)/shard_map/ppermute | solution.py:9
  111.2 54.2 %collective-permute-start.16 = (bf16[1,128,2048]{1,2,0:T(8,128)(2,1)S(1)}, bf16[1,128,2048]{1,2,0:T(8,128)(2,1)}, u32[]{:S(2)}, u32[]{:S(2)}) collective-permute-start(bf16[1,128,2048]{1,2,0:T(8,128)(2,1)S(1)} %copy.160), channel_id=1, source_target_pairs={{0,24},{2,26},{4,28},{6,30},{8,0},{10,2},{12,4},{14,6},{16,8},{18,... | collective-permute-start | bytes 1572872 | tf_op jit(solution)/shard_map/ppermute | solution.py:9
  138.5 31.2 %collective-permute-start.12 = (bf16[1,128,2048]{1,2,0:T(8,128)(2,1)S(1)}, bf16[1,128,2048]{1,2,0:T(8,128)(2,1)S(1)}, u32[]{:S(2)}, u32[]{:S(2)}) collective-permute-start(bf16[1,128,2048]{1,2,0:T(8,128)(2,1)S(1)} %copy.160), channel_id=1, source_target_pairs={{0,8},{2,10},{4,12},{6,14},{8,16},{10,18},{12,20},{14,22},{16,24},... | collective-permute-start | bytes 1572872 | tf_op jit(solution)/shard_map/ppermute | solution.py:9
  193.4 146.7 %collective-permute-start.19 = (bf16[128,2048]{0,1:T(8,128)(2,1)}, bf16[128,2048]{0,1:T(8,128)(2,1)}, u32[]{:S(2)}, u32[]{:S(2)}) collective-permute-start(bf16[128,2048]{0,1:T(8,128)(2,1)} %bitcast.17), channel_id=1, source_target_pairs={{0,28},{2,30},{4,0},{6,2},{8,4},{10,6},{12,8},{14,10},{16,12},{18,... | collective-permute-start | bytes 1572872 | tf_op jit(solution)/shard_map/ppermute | solution.py:9
  254.0 88.6 %collective-permute-start.20 = (bf16[128,2048]{0,1:T(8,128)(2,1)}, bf16[128,2048]{0,1:T(8,128)(2,1)}, u32[]{:S(2)}, u32[]{:S(2)}) collective-permute-start(bf16[128,2048]{0,1:T(8,128)(2,1)} %bitcast.152), channel_id=1, source_target_pairs={{0,26},{2,28},{4,30},{6,0},{8,2},{10,4},{12,6},{14,8},{16,10},{18,... | collective-permute-start | bytes 1572872 | tf_op jit(solution)/shard_map/ppermute | solution.py:9
  254.0 126.4 %collective-permute-start.18 = (bf16[128,2048]{0,1:T(8,128)(2,1)}, bf16[128,2048]{0,1:T(8,128)(2,1)}, u32[]{:S(2)}, u32[]{:S(2)}) collective-permute-start(bf16[128,2048]{0,1:T(8,128)(2,1)} %bitcast.151), channel_id=1, source_target_pairs={{0,30},{2,0},{4,2},{6,4},{8,6},{10,8},{12,10},{14,12},{16,14},{18,... | collective-permute-start | bytes 1572872 | tf_op jit(solution)/shard_map/ppermute | solution.py:9
  324.2 59.1 %collective-permute-start.23 = (bf16[128,2048]{1,0:T(8,128)(2,1)}, bf16[128,2048]{1,0:T(8,128)(2,1)}, u32[]{:S(2)}, u32[]{:S(2)}) collective-permute-start(bf16[128,2048]{1,0:T(8,128)(2,1)} %copy.132), channel_id=1, source_target_pairs={{0,8},{2,10},{4,12},{6,14},{8,16},{10,18},{12,20},{14,22},{16,24},... | collective-permute-start | bytes 1572872 | tf_op jit(solution)/shard_map/ppermute | solution.py:9
  324.2 93.9 %collective-permute-start.26 = (bf16[128,2048]{1,0:T(8,128)(2,1)}, bf16[128,2048]{1,0:T(8,128)(2,1)}, u32[]{:S(2)}, u32[]{:S(2)}) collective-permute-start(bf16[128,2048]{1,0:T(8,128)(2,1)} %copy.140), channel_id=1, source_target_pairs={{0,8},{2,10},{4,12},{6,14},{8,16},{10,18},{12,20},{14,22},{16,24},... | collective-permute-start | bytes 1572872 | tf_op jit(solution)/shard_map/ppermute | solution.py:9
  340.1 52.3 %collective-permute-start.22 = (bf16[128,2048]{1,0:T(8,128)(2,1)}, bf16[128,2048]{1,0:T(8,128)(2,1)}, u32[]{:S(2)}, u32[]{:S(2)}) collective-permute-start(bf16[128,2048]{1,0:T(8,128)(2,1)} %copy.130), channel_id=1, source_target_pairs={{0,16},{2,18},{4,20},{6,22},{8,24},{10,26},{12,28},{14,30},{16,0},... | collective-permute-start | bytes 1572872 | tf_op jit(solution)/shard_map/ppermute | solution.py:9
  342.6 75.5 %collective-permute-start.25 = (bf16[128,2048]{1,0:T(8,128)(2,1)}, bf16[128,2048]{1,0:T(8,128)(2,1)}, u32[]{:S(2)}, u32[]{:S(2)}) collective-permute-start(bf16[128,2048]{1,0:T(8,128)(2,1)} %copy.138), channel_id=1, source_target_pairs={{0,16},{2,18},{4,20},{6,22},{8,24},{10,26},{12,28},{14,30},{16,0},... | collective-permute-start | bytes 1572872 | tf_op jit(solution)/shard_map/ppermute | solution.py:9
  380.4 35.3 %collective-permute-start.21 = (bf16[128,2048]{1,0:T(8,128)(2,1)}, bf16[128,2048]{1,0:T(8,128)(2,1)}, u32[]{:S(2)}, u32[]{:S(2)}) collective-permute-start(bf16[128,2048]{1,0:T(8,128)(2,1)} %copy.127), channel_id=1, source_target_pairs={{0,24},{2,26},{4,28},{6,30},{8,0},{10,2},{12,4},{14,6},{16,8},{18,... | collective-permute-start | bytes 1572872 | tf_op jit(solution)/shard_map/ppermute | solution.py:9
  383.3 43.5 %collective-permute-start.24 = (bf16[128,2048]{1,0:T(8,128)(2,1)}, bf16[128,2048]{1,0:T(8,128)(2,1)S(1)}, u32[]{:S(2)}, u32[]{:S(2)}) collective-permute-start(bf16[128,2048]{1,0:T(8,128)(2,1)} %copy.135), channel_id=1, source_target_pairs={{0,24},{2,26},{4,28},{6,30},{8,0},{10,2},{12,4},{14,6},{16,8},{18,... | collective-permute-start | bytes 1572872 | tf_op jit(solution)/shard_map/ppermute | solution.py:9
  (33 other events, 513.7 us)
Sparse Core Ops, SparseCore 0:
  17.5 293.5 reduce-scatter.1
where the time goes:
time: 442 us; the launch traced here: 440 us
  starting transfers between devices  180 us (41%)
  waiting for transfers between devices  128 us (29%)
  matrix products  64.5 us (15%)
  local copies, waits for them, and re-layouts  35.7 us (8%)
  other arithmetic  14.6 us (3%)
  between operations  14.6 us (3%)
    ppermute x27, starting transfers between devices, shifted(): lax.ppermute(shard, axis, [(i, (i + by) % count) for i in range(count)])  180 us
    ppermute x27, waiting for transfers between devices, shifted(): lax.ppermute(shard, axis, [(i, (i + by) % count) for i in range(count)])  128 us
    dot_general x4, matrix products, block_core(): jnp.einsum('ahd,bhd->hab', grad_split, value_heads, preferred_element_typ...  16.7 us
    dot_general x4, matrix products, block_core(): jnp.einsum('hab,ahd->bhd', probs_low, grad_split, preferred_element_type=...  14.3 us
    unnamed x66, local copies, waits for them, and re-layouts  9.65 us
    dot_general x1, matrix products, per_device(): lax.dot_general(columns, cotangent, (((0,), (0,)), ((), ())), preferred_e...  9.18 us
  transfers between devices with their start and end apart: 28, of which 9 were waited for; matrix products, arithmetic and copies ran while one was open for 23% of the time, Pallas kernels for 0%

commit v1 on v0

--- a/solution.py
+++ b/solution.py
@@ -1,6 +1,10 @@
+import functools
+
 import jax
 import jax.numpy as jnp
 from jax import lax
+from jax.experimental import pallas as pl
+from jax.experimental.pallas import tpu as pltpu
 from jax.sharding import PartitionSpec as P
 
 
@@ -67,7 +71,7 @@
     return (parts[0], parts[1].astype(jnp.bfloat16), parts[2].astype(jnp.bfloat16))
 
 
-def per_device(block_pos, queries, keys, values, attn_out, log_sums, grad_out, out_weight):
+def grid_per_device(block_pos, queries, keys, values, attn_out, log_sums, grad_out, out_weight):
     dev_count = lax.axis_size("seq")
     grid_side = 4 + 4 * (dev_count // 64)
     my_index = lax.axis_index("seq")
@@ -159,6 +163,365 @@
     )
 
 
+MESH = pl.DeviceIdType.MESH
+ANY = pl.BlockSpec(memory_space=pl.ANY)
+
+
+def enter(count, side, cores, me, core):
+    barrier = pltpu.get_barrier_semaphore()
+    plane = me // side * side
+    for step in range(1, count):
+        pl.semaphore_signal(
+            barrier, inc=1, device_id=(lax.rem(me + step, count), core), device_id_type=MESH
+        )
+    total = count - 1
+    for turn in range(1, cores):
+        for step in range(side):
+            peer = (plane + step, lax.rem(core + turn, cores))
+            pl.semaphore_signal(barrier, inc=1, device_id=peer, device_id_type=MESH)
+            total += 1
+    pl.semaphore_wait(barrier, total)
+
+
+def gather_kernel(
+    count, side, cores, dim,
+    q_in, k_in, v_in, g_in, s_in, a_in, b_in,
+    q_out, k_out, v_out, g_out, s_out, a_out, b_out,
+    send, recv, plane_send, plane_recv, local,
+):
+    me = lax.axis_index("seq")
+    core = lax.axis_index("dp")
+    column = lax.rem(me, side)
+    plane = me - column
+    half = b_out.shape[2]
+    enter(count, side, cores, me, core)
+
+    def head_pieces(head, owner):
+        cut = pl.ds(pl.multiple_of(head * dim, dim), dim)
+        pairs = [
+            (source.at[:, cut], target.at[owner])
+            for source, target in ((q_in, q_out), (k_in, k_out), (v_in, v_out), (g_in, g_out))
+        ]
+        return pairs + [(s_in.at[head], s_out.at[owner])]
+
+    def plane_pieces(to_column, to_core, slot):
+        pairs = []
+        for part in range(side):
+            cut = pl.ds(pl.multiple_of((part * side + to_column) * dim, dim), dim)
+            pairs.append((a_in.at[:, cut], a_out.at[slot, :, pl.ds(part * dim, dim)]))
+        cut = pl.ds(pl.multiple_of(to_core * half, half), half)
+        return pairs + [(b_in.at[:, cut], b_out.at[slot])]
+
+    def head_copies(head, owner, out_index, in_index, device):
+        return [
+            pltpu.make_async_remote_copy(
+                source, target, send.at[at, out_index], recv.at[at, in_index],
+                device_id=device, device_id_type=MESH,
+            )
+            for at, (source, target) in enumerate(head_pieces(head, owner))
+        ]
+
+    def plane_copies(to_column, to_core, slot, out_index, in_index, device):
+        return [
+            pltpu.make_async_remote_copy(
+                source, target, plane_send.at[at, out_index], plane_recv.at[at, in_index],
+                device_id=device, device_id_type=MESH,
+            )
+            for at, (source, target) in enumerate(plane_pieces(to_column, to_core, slot))
+        ]
+
+    own_slot = column * cores + core
+    owns = [
+        pltpu.make_async_copy(source, target, local.at[at])
+        for at, (source, target) in enumerate(
+            head_pieces(me, me) + plane_pieces(column, core, own_slot)
+        )
+    ]
+    members = side * cores
+
+    def plane_peer(step):
+        slot = lax.rem(own_slot + step, members)
+        return slot, slot // cores, lax.rem(slot, cores)
+
+    @pl.loop(1, count)
+    def _(step):
+        peer = lax.rem(me + step, count)
+        for copy in head_copies(peer, me, step, me, (peer, core)):
+            copy.start()
+
+    for copy in owns:
+        copy.start()
+
+    @pl.loop(1, members)
+    def _(step):
+        slot, to_column, to_core = plane_peer(step)
+        for copy in plane_copies(
+            to_column, to_core, own_slot, step, own_slot, (plane + to_column, to_core)
+        ):
+            copy.start()
+
+    for copy in owns:
+        copy.wait()
+
+    @pl.loop(1, count)
+    def _(step):
+        peer = lax.rem(me + step, count)
+        for copy in head_copies(peer, me, step, me, (peer, core)):
+            copy.wait_send()
+        for copy in head_copies(me, peer, step, peer, (peer, core)):
+            copy.wait_recv()
+
+    @pl.loop(1, members)
+    def _(step):
+        slot, to_column, to_core = plane_peer(step)
+        device = (plane + to_column, to_core)
+        for copy in plane_copies(to_column, to_core, own_slot, step, own_slot, device):
+            copy.wait_send()
+        for copy in plane_copies(column, core, slot, step, slot, device):
+            copy.wait_recv()
+
+
+def return_kernel(
+    count, side, cores, dim,
+    q_in, k_in, v_in, w_in,
+    q_out, k_out, v_out, w_out,
+    send, recv, line_send, line_recv, local,
+):
+    me = lax.axis_index("seq")
+    core = lax.axis_index("dp")
+    row = me // side
+    column = lax.rem(me, side)
+    enter(count, side, 1, me, core)
+
+    def pieces(owner, head):
+        cut = pl.ds(pl.multiple_of(head * dim, dim), dim)
+        return [
+            (source.at[owner], target.at[:, cut])
+            for source, target in ((q_in, q_out), (k_in, k_out), (v_in, v_out))
+        ]
+
+    def copies(owner, head, out_index, in_index, device):
+        return [
+            pltpu.make_async_remote_copy(
+                source, target, send.at[at, out_index], recv.at[at, in_index],
+                device_id=device, device_id_type=MESH,
+            )
+            for at, (source, target) in enumerate(pieces(owner, head))
+        ]
+
+    def line_copy(to_row, slot, out_index, in_index, device):
+        return pltpu.make_async_remote_copy(
+            w_in.at[to_row], w_out.at[slot], line_send.at[out_index], line_recv.at[in_index],
+            device_id=device, device_id_type=MESH,
+        )
+
+    owns = [
+        pltpu.make_async_copy(source, target, local.at[at])
+        for at, (source, target) in enumerate(
+            pieces(me, me) + [(w_in.at[row], w_out.at[row])]
+        )
+    ]
+
+    for step in range(1, side):
+        to_row = lax.rem(row + step, side)
+        line_copy(to_row, row, step, row, (to_row * side + column, core)).start()
+
+    @pl.loop(1, count)
+    def _(step):
+        peer = lax.rem(me + step, count)
+        for copy in copies(peer, me, step, me, (peer, core)):
+            copy.start()
+
+    for copy in owns:
+        copy.start()
+    for copy in owns:
+        copy.wait()
+
+    for step in range(1, side):
+        to_row = lax.rem(row + step, side)
+        device = (to_row * side + column, core)
+        line_copy(to_row, row, step, row, device).wait_send()
+        line_copy(row, to_row, step, to_row, device).wait_recv()
+
+    @pl.loop(1, count)
+    def _(step):
+        peer = lax.rem(me + step, count)
+        for copy in copies(peer, me, step, me, (peer, core)):
+            copy.wait_send()
+        for copy in copies(me, peer, step, peer, (peer, core)):
+            copy.wait_recv()
+
+
+def head_kernel(
+    tile, scaling, table, q_in, k_in, v_in, g_in, s_in, q_out, k_out, v_out,
+    q_row, k_row, v_row, g_row, s_row, dq, dk, dv,
+):
+    blocks = table.shape[0]
+    length, _ = q_in.shape
+    half = length // blocks
+    lanes = 2 * half
+    side_of = lax.broadcasted_iota(jnp.int32, s_row.shape[1:], 1) // half
+    for block in range(blocks):
+        place = table[block]
+        source = pl.ds(block * half, half)
+        target = pl.ds(pl.multiple_of(place * half, half), half)
+        for raw, ordered in ((q_in, q_row), (k_in, k_row), (v_in, v_row), (g_in, g_row)):
+            ordered[target, :] = raw[source, :]
+        stats = s_in[block // 2]
+        turned = pltpu.roll(stats, half, 1)
+        parity = place % 2
+        chosen = jnp.where(parity == block % 2, stats, turned)
+        s_row[place // 2] = jnp.where(side_of == parity, chosen, s_row[place // 2])
+    tiles = length // tile
+    per_tile = tile // lanes
+    dq[...] = jnp.zeros_like(dq)
+
+    def pair(i, j, diagonal, sums):
+        key_cut = pl.ds(j * tile, tile)
+        query_cut = pl.ds(pl.multiple_of(i * tile, tile), tile)
+        k_tile, v_tile = k_row[key_cut, :], v_row[key_cut, :]
+        q_tile, g_tile = q_row[query_cut, :], g_row[query_cut, :]
+        log_line = jnp.concatenate(
+            [s_row[i * per_tile + m, 0:1, :] for m in range(per_tile)], axis=1
+        )
+        delta_line = jnp.concatenate(
+            [s_row[i * per_tile + m, 1:2, :] for m in range(per_tile)], axis=1
+        )
+        by_rows = (((1,), (1,)), ((), ()))
+        scores = lax.dot_general(k_tile, q_tile, by_rows, preferred_element_type=jnp.float32)
+        probs = jnp.exp(scores * scaling - log_line)
+        if diagonal:
+            key_at = lax.broadcasted_iota(jnp.int32, (tile, tile), 0)
+            query_at = lax.broadcasted_iota(jnp.int32, (tile, tile), 1)
+            probs = jnp.where(key_at <= query_at, probs, 0.0)
+        dprobs = lax.dot_general(v_tile, g_tile, by_rows, preferred_element_type=jnp.float32)
+        dscores = (probs * (dprobs - delta_line)).astype(jnp.bfloat16)
+        dv_sum = sums[1] + jnp.dot(
+            probs.astype(jnp.bfloat16), g_tile, preferred_element_type=jnp.float32
+        )
+        dk_sum = sums[0] + jnp.dot(dscores, q_tile, preferred_element_type=jnp.float32)
+        dq[query_cut, :] += lax.dot_general(
+            dscores, k_tile, (((0,), (0,)), ((), ())), preferred_element_type=jnp.float32
+        )
+        return dk_sum, dv_sum
+
+    for j in range(tiles):
+        zero = jnp.zeros((tile, dq.shape[1]), jnp.float32)
+        sums = pair(j, j, True, (zero, zero))
+        if j + 1 < tiles:
+            sums = lax.fori_loop(
+                j + 1, tiles, lambda i, carry: pair(i, j, False, carry), sums
+            )
+        dk[pl.ds(j * tile, tile), :] = sums[0]
+        dv[pl.ds(j * tile, tile), :] = sums[1]
+    for block in range(blocks):
+        place = table[block]
+        target = pl.ds(block * half, half)
+        source = pl.ds(pl.multiple_of(place * half, half), half)
+        q_out[target, :] = (dq[source, :] * scaling).astype(q_out.dtype)
+        k_out[target, :] = (dk[source, :] * scaling).astype(k_out.dtype)
+        v_out[target, :] = dv[source, :].astype(v_out.dtype)
+
+
+def head_per_device(
+    side, cores, block_pos, queries, keys, values, attn_out, log_sums, grad_out, out_weight
+):
+    count = lax.axis_size("seq")
+    rows = queries.shape[1]
+    width = queries.shape[2]
+    heads = log_sums.shape[1]
+    dim = width // heads
+    scaling = dim ** (-0.5)
+    out_width = grad_out.shape[2]
+    share = out_width // cores
+    length = count * rows
+    low = jnp.bfloat16
+    cotangent = grad_out[0]
+    grad_heads = lax.dot_general(
+        cotangent, out_weight, (((1,), (1,)), ((), ())), preferred_element_type=jnp.float32
+    ).astype(low)
+    deltas = jnp.einsum(
+        "ahd,ahd->ha",
+        grad_heads.reshape(rows, heads, dim),
+        attn_out[0].reshape(rows, heads, dim),
+        preferred_element_type=jnp.float32,
+    )
+    stats = jnp.stack([log_sums[0], deltas], axis=1)
+    stats = jnp.pad(stats, ((0, 0), (0, 6), (0, 0)))
+    shapes = [jax.ShapeDtypeStruct((count, rows, dim), low)] * 4 + [
+        jax.ShapeDtypeStruct((count, 8, rows), jnp.float32),
+        jax.ShapeDtypeStruct((side * cores, rows, side * dim), low),
+        jax.ShapeDtypeStruct((side * cores, rows, share), low),
+    ]
+    dma = pltpu.SemaphoreType.DMA
+    members = side * cores
+    q_all, k_all, v_all, g_all, s_all, a_all, b_all = pl.pallas_call(
+        functools.partial(gather_kernel, count, side, cores, dim),
+        out_shape=shapes,
+        in_specs=[ANY] * 7,
+        out_specs=[ANY] * 7,
+        scratch_shapes=[
+            dma((5, count)), dma((5, count)),
+            dma((side + 1, members)), dma((side + 1, members)), dma((side + 6,)),
+        ],
+        compiler_params=pltpu.CompilerParams(collective_id=0, has_side_effects=True),
+    )(queries[0], keys[0], values[0], grad_heads, stats, attn_out[0], cotangent)
+    partial = lax.dot_general(
+        a_all.reshape(members * rows, side * dim),
+        b_all.reshape(members * rows, share),
+        (((0,), (0,)), ((), ())),
+        preferred_element_type=jnp.float32,
+    ).astype(low)
+    tile = min(512, length)
+    vmem = pl.BlockSpec(memory_space=pltpu.VMEM)
+    wide = (length, dim)
+    parts = pl.pallas_call(
+        functools.partial(head_kernel, tile, scaling),
+        out_shape=[jax.ShapeDtypeStruct(wide, low)] * 3,
+        in_specs=[pl.BlockSpec(memory_space=pltpu.SMEM)] + [vmem] * 5,
+        out_specs=[vmem] * 3,
+        scratch_shapes=[pltpu.VMEM(wide, low)] * 4
+        + [pltpu.VMEM((count, 8, rows), jnp.float32)]
+        + [pltpu.VMEM(wide, jnp.float32)] * 3,
+        compiler_params=pltpu.CompilerParams(vmem_limit_bytes=56 * 1024 * 1024),
+    )(
+        block_pos[0], q_all.reshape(wide), k_all.reshape(wide), v_all.reshape(wide),
+        g_all.reshape(wide), s_all,
+    )
+    pieces = [part.reshape(count, rows, dim) for part in parts]
+    grad_queries, grad_keys, grad_values, w_all = pl.pallas_call(
+        functools.partial(return_kernel, count, side, cores, dim),
+        out_shape=[jax.ShapeDtypeStruct((rows, width), low)] * 3
+        + [jax.ShapeDtypeStruct((side, dim, share), low)],
+        in_specs=[ANY] * 4,
+        out_specs=[ANY] * 4,
+        scratch_shapes=[
+            dma((3, count)), dma((3, count)), dma((side,)), dma((side,)), dma((4,)),
+        ],
+        compiler_params=pltpu.CompilerParams(collective_id=1, has_side_effects=True),
+    )(*pieces, partial.reshape(side, dim, share))
+    weight_share = jnp.sum(w_all.astype(jnp.float32), axis=0).astype(low)
+    weight_share = lax.all_gather(weight_share, "dp", axis=1, tiled=True).astype(jnp.float32)
+    return grad_queries[None], grad_keys[None], grad_values[None], weight_share
+
+
+def make_per_device(mesh):
+    count = mesh.shape["seq"]
+    cores = mesh.shape["dp"]
+    side = int(round(count ** 0.5))
+
+    def per_device(block_pos, queries, keys, values, attn_out, log_sums, grad_out, out_weight):
+        heads = log_sums.shape[1]
+        arguments = (
+            block_pos, queries, keys, values, attn_out, log_sums, grad_out, out_weight
+        )
+        if heads == count and side * side == count:
+            return head_per_device(side, cores, *arguments)
+        return grid_per_device(*arguments)
+
+    return per_device
+
+
 def solution(mesh):
     in_specs = (
         P("dp", None),
@@ -172,5 +535,5 @@
     )
     out_specs = (P("dp", "seq", None), P("dp", "seq", None), P("dp", "seq", None), P("seq", None))
     return jax.shard_map(
-        per_device, mesh=mesh, in_specs=in_specs, out_specs=out_specs, check_vma=False
-    )
+        make_per_device(mesh), mesh=mesh, in_specs=in_specs, out_specs=out_specs, check_vma=False
+    )

time: 442 us -> 164 us (0.37)
  the two profiles are of different devices: /device:TPU:3 before, /device:TPU:15 now
where the time goes in v1:
time: 164 us
  Pallas kernels  145 us (88%)
  matrix products  9.95 us (6%)
  other arithmetic  3.58 us (2%)
  local copies, waits for them, and re-layouts  2.74 us (2%)
  blocking collectives  2.54 us (2%)
    pallas_call x1, Pallas kernels, head_per_device(): pl.pallas_call(functools.partial(gather_kernel, count, side, cores, dim),...  67.2 us
    pallas_call x1, Pallas kernels, head_per_device(): pl.pallas_call(functools.partial(return_kernel, count, side, cores, dim),...  65.5 us
    pallas_call x1, Pallas kernels, head_per_device(): pl.pallas_call(functools.partial(head_kernel, tile, scaling), out_shape=[...  11.9 us
    dot_general x1, matrix products, head_per_device(): lax.dot_general(cotangent, out_weight, (((1,), (1,)), ((), ())), preferre...  6.49 us
    dot_general x1, matrix products, head_per_device(): lax.dot_general(a_all.reshape(members * rows, side * dim), b_all.reshape(...  3.46 us

profile of v1, /device:TPU:15, one launch (start us, length us, event | category | flops | bytes accessed | tf_op | source)
XLA Modules:
  0.0 164.2 jit_solution(8712840615638673912)
XLA Ops:
  0.6 0.0 copy-start.1
  0.6 6.5 %convolution_convert_fusion.g_in = bf16[128,2048]{1,0:T(8,128)(2,1)S(1)} fusion(bf16[2048,2048]{1,0:T(8,128)(2,1)} %param.15, bf16[1,128,2048]{2,1,0:T(8,128)(2,1)} %param.14), kind=kOutput, calls=%fused_computation | convolution fusion | flops 1074003968 | bytes 9437184 | tf_op jit(solution)/shard_map/dot_general | solution.py:440
  7.1 0.0 copy-start
  7.2 0.0 copy-start.6
  7.2 0.1 copy.22
  7.3 0.1 copy.23
  7.4 0.4 fusion
  7.8 0.1 copy.19
  7.8 0.1 copy-done.6
  7.9 0.6 select_maximum_fusion.s_in
  8.5 67.2 %shard_map.111 = (bf16[16,128,128]{2,1,0:T(8,128)(2,1)}, bf16[16,128,128]{2,1,0:T(8,128)(2,1)}, bf16[16,128,128]{2,1,0:T(8,128)(2,1)}, bf16[16,128,128]{2,1,0:T(...) custom-call(bf16[128,2048]{1,0:T(8,128)(2,1)} %bitcast.42, ...), custom_call_target="tpu_custom_call" | custom-call | tf_op jit(solution)/shard_map/pallas_call | solution.py:458
  75.7 0.0 copy-start.2
  75.8 11.9 %shard_map.112 = (bf16[2048,128]{1,0:T(8,128)(2,1)}, bf16[2048,128]{1,0:T(8,128)(2,1)}, bf16[2048,128]{1,0:T(8,128)(2,1)}) custom-call(s32[32]{0:T(128)} %bitcast.57, bf16[2048,128]{1,0:T(8,128)(2,1)} %bitcast.48, bf16[2048,128]{1,0:T(8,128)(2,1)} %bitcast.49, bf16[2048,128]{1,0:T(8,128)(2,1)} %bitcast.50, bf16[2048,128]{1,0:T(8,128)(2,1)} %bitcast.51, ...), custom_call_target="tpu_custom_call" | custom-call | tf_op jit(solution)/shard_map/pallas_call | solution.py:478
  87.7 3.5 %bitcast_convert_fusion = bf16[512,1024]{1,0:T(8,128)(2,1)} fusion(bf16[8,128,512]{2,1,0:T(8,128)(2,1)} %get-tuple-element.26, bf16[8,128,1024]{2,1,0:T(8,128)(2,1)S(1)} %copy-done.2), kind=kOutput, calls=%fused_computation.1 | convolution fusion | flops 1074266112 | bytes 4194304 | tf_op jit(solution)/shard_map/dot_general | solution.py:469
  91.2 65.5 %shard_map.113 = (bf16[128,2048]{1,0:T(8,128)(2,1)}, bf16[128,2048]{1,0:T(8,128)(2,1)}, bf16[128,2048]{1,0:T(8,128)(2,1)}, bf16[4,128,1024]{2,1,0:T(8,128)(2,1)}) custom-call(bf16[16,128,128]{2,1,0:T(8,128)(2,1)} %bitcast.45, bf16[16,128,128]{2,1,0:T(8,128)(2,1)} %bitcast.46, bf16[16,128,128]{2,1,0:T(8,128)(2,1)} %bitcast.47, bf16[4,128,1024]{2,1,0:T(8,128)(2,1)} %bitcast.36), custom_call_target="tpu_custom_call" | custom-call | tf_op jit(solution)/shard_map/pallas_call | solution.py:492
  156.7 0.0 copy-start.5
  156.7 0.0 copy-start.4
  156.7 1.5 reduce_sum.12
  158.2 2.5 %all_gather.3 = bf16[128,2048]{1,0:T(8,128)(2,1)S(1)} all-gather(bf16[128,1024]{1,0:T(8,128)(2,1)S(1)} %reduce_sum.12), channel_id=1, replica_groups=mesh['seq'=16,'dp'=2] {'dp'}, dimensions={1}, use_global_device_ids=true | all-gather | bytes 786432 | tf_op jit(solution)/shard_map/all_gather | solution.py:504
  160.8 1.1 convert_element_type.15
  161.8 0.8 copy.27
  162.6 0.8 copy.28
  163.4 0.0 copy-done.3
  163.4 0.8 copy.29
  (6 shorter events, 0.0 us)
Async XLA Ops:
  0.6 6.7 %copy-start.1 = (bf16[1,128,2048]{2,1,0:T(8,128)(2,1)S(1)}, bf16[1,128,2048]{2,1,0:T(8,128)(2,1)}, u32[]{:S(2)}) copy-start(bf16[1,128,2048]{2,1,0:T(8,128)(2,1)} %param.12) | copy-start | bytes 1572868
  7.1 1.4 copy-start
  7.2 0.7 copy-start.6
  75.7 11.9 %copy-start.2 = (bf16[8,128,1024]{2,1,0:T(8,128)(2,1)S(1)}, bf16[8,128,1024]{2,1,0:T(8,128)(2,1)}, u32[]{:S(2)}) copy-start(bf16[8,128,1024]{2,1,0:T(8,128)(2,1)} %get-tuple-element.27) | copy-start | bytes 6291460
  156.7 5.2 %copy-start.5 = (bf16[128,2048]{1,0:T(8,128)(2,1)S(1)}, bf16[128,2048]{1,0:T(8,128)(2,1)}, u32[]{:S(2)}) copy-start(bf16[128,2048]{1,0:T(8,128)(2,1)} %get-tuple-element.28) | copy-start | bytes 1572868
  156.7 5.9 %copy-start.4 = (bf16[128,2048]{1,0:T(8,128)(2,1)S(1)}, bf16[128,2048]{1,0:T(8,128)(2,1)}, u32[]{:S(2)}) copy-start(bf16[128,2048]{1,0:T(8,128)(2,1)} %get-tuple-element.29) | copy-start | bytes 1572868
  158.2 5.2 %copy-start.3 = (bf16[128,2048]{1,0:T(8,128)(2,1)S(1)}, bf16[128,2048]{1,0:T(8,128)(2,1)}, u32[]{:S(2)}) copy-start(bf16[128,2048]{1,0:T(8,128)(2,1)} %get-tuple-element.30) | copy-start | bytes 1572868

commit v2 on v0

--- a/solution.py
+++ b/solution.py
@@ -1,6 +1,10 @@
+import functools
+
 import jax
 import jax.numpy as jnp
 from jax import lax
+from jax.experimental import pallas as pl
+from jax.experimental.pallas import tpu as pltpu
 from jax.sharding import PartitionSpec as P
 
 
@@ -67,7 +71,7 @@
     return (parts[0], parts[1].astype(jnp.bfloat16), parts[2].astype(jnp.bfloat16))
 
 
-def per_device(block_pos, queries, keys, values, attn_out, log_sums, grad_out, out_weight):
+def grid_per_device(block_pos, queries, keys, values, attn_out, log_sums, grad_out, out_weight):
     dev_count = lax.axis_size("seq")
     grid_side = 4 + 4 * (dev_count // 64)
     my_index = lax.axis_index("seq")
@@ -159,6 +163,422 @@
     )
 
 
+MESH = pl.DeviceIdType.MESH
+ANY = pl.BlockSpec(memory_space=pl.ANY)
+
+
+def enter(count, side, cores, me, core):
+    barrier = pltpu.get_barrier_semaphore()
+    plane = me // side * side
+    for step in range(1, count):
+        pl.semaphore_signal(
+            barrier, inc=1, device_id=(lax.rem(me + step, count), core), device_id_type=MESH
+        )
+    total = count - 1
+    for turn in range(1, cores):
+        for step in range(side):
+            peer = (plane + step, lax.rem(core + turn, cores))
+            pl.semaphore_signal(barrier, inc=1, device_id=peer, device_id_type=MESH)
+            total += 1
+    pl.semaphore_wait(barrier, total)
+
+
+def fused_kernel(
+    count, side, cores, dim, tile, scaling,
+    places, q_in, k_in, v_in, a_in, b_in, l_in, w_in,
+    q_out, k_out, v_out, w_out,
+    q_all, k_all, v_all, g_all, s_all, a_all, b_all,
+    a_own, b_own, l_own, w_own, g_own, s_own,
+    q_row, k_row, v_row, g_row, s_row, dq, dk, dv,
+    q_back, k_back, v_back, w_part, w_line, w_half,
+    send, recv, plane_send, plane_recv, line_send, line_recv,
+    back_send, back_recv, half_send, half_recv, local,
+):
+    me = lax.axis_index("seq")
+    core = lax.axis_index("dp")
+    column = lax.rem(me, side)
+    plane = me - column
+    row = me // side
+    half = b_all.shape[2]
+    members = side * cores
+    own_slot = column * cores + core
+    low = jnp.bfloat16
+
+    loads = [
+        pltpu.make_async_copy(source, target, local.at[at])
+        for at, (source, target) in enumerate(
+            [(b_in, b_own), (w_in, w_own), (a_in, a_own), (l_in, l_own)]
+        )
+    ]
+    for copy in loads:
+        copy.start()
+    enter(count, side, cores, me, core)
+
+    def head_cut(head):
+        return pl.ds(pl.multiple_of(head * dim, dim), dim)
+
+    rows = a_all.shape[1]
+
+    def owner_blocks(owner):
+        return pl.ds(owner * 2, 2)
+
+    def remote(source, target, sender, receiver, device):
+        return pltpu.make_async_remote_copy(
+            source, target, sender, receiver, device_id=device, device_id_type=MESH
+        )
+
+    def row_pieces(head, owner):
+        cut = head_cut(head)
+        return [
+            (q_in.at[:, :, cut], q_all.at[owner_blocks(owner)]),
+            (k_in.at[:, :, cut], k_all.at[owner_blocks(owner)]),
+            (v_in.at[:, :, cut], v_all.at[owner_blocks(owner)]),
+        ]
+
+    def grad_pieces(head, owner):
+        return [
+            (g_own.at[head], g_all.at[owner_blocks(owner)]),
+            (s_own.at[head], s_all.at[owner_blocks(owner)]),
+        ]
+
+    def head_copies(pieces, base, out_index, in_index, device):
+        return [
+            remote(source, target, send.at[base + at, out_index], recv.at[base + at, in_index], device)
+            for at, (source, target) in enumerate(pieces)
+        ]
+
+    def plane_pieces(to_column, to_core, slot):
+        pairs = []
+        for part in range(side):
+            cut = head_cut(part * side + to_column)
+            pairs.append((a_in.at[:, cut], a_all.at[slot, :, pl.ds(part * dim, dim)]))
+        cut = pl.ds(pl.multiple_of(to_core * half, half), half)
+        return pairs + [(b_in.at[:, cut], b_all.at[slot])]
+
+    def plane_copies(to_column, to_core, slot, out_index, in_index, device):
+        return [
+            remote(source, target, plane_send.at[at, out_index], plane_recv.at[at, in_index], device)
+            for at, (source, target) in enumerate(plane_pieces(to_column, to_core, slot))
+        ]
+
+    def plane_peer(step):
+        slot = lax.rem(own_slot + step, members)
+        return slot, slot // cores, lax.rem(slot, cores)
+
+    def line_copy(to_row, slot, out_index, in_index, device):
+        return remote(
+            w_part.at[to_row], w_line.at[slot], line_send.at[out_index],
+            line_recv.at[in_index], device,
+        )
+
+    def back_pieces(owner, head):
+        cut = head_cut(head)
+        return [
+            (source.at[owner], target.at[:, cut])
+            for source, target in ((q_back, q_out), (k_back, k_out), (v_back, v_out))
+        ]
+
+    def back_copies(owner, head, out_index, in_index, device):
+        return [
+            remote(source, target, back_send.at[at, out_index], back_recv.at[at, in_index], device)
+            for at, (source, target) in enumerate(back_pieces(owner, head))
+        ]
+
+    @pl.loop(1, count)
+    def _(step):
+        peer = lax.rem(me + step, count)
+        for copy in head_copies(row_pieces(peer, me), 0, step, me, (peer, core)):
+            copy.start()
+
+    @pl.loop(1, members)
+    def _(step):
+        slot, to_column, to_core = plane_peer(step)
+        for copy in plane_copies(
+            to_column, to_core, own_slot, step, own_slot, (plane + to_column, to_core)
+        ):
+            copy.start()
+
+    owns = [
+        pltpu.make_async_copy(source, target, local.at[4 + at])
+        for at, (source, target) in enumerate(
+            row_pieces(me, me) + plane_pieces(column, core, own_slot)
+        )
+    ]
+    for copy in owns:
+        copy.start()
+    for copy in loads:
+        copy.wait()
+
+    by_rows = (((1,), (1,)), ((), ()))
+    by_columns = (((0,), (0,)), ((), ()))
+    stat_rows = s_own.shape[2:]
+    block_rows = rows // 2
+    stat_at = lax.broadcasted_iota(jnp.int32, stat_rows, 0)
+    early_half = lax.broadcasted_iota(jnp.int32, stat_rows, 1) < block_rows
+    log_row = stat_at < 1
+
+    @pl.loop(1, count + 1)
+    def _(step):
+        head = lax.rem(me + step, count)
+        grads = lax.dot_general(
+            b_own[...], w_own[head_cut(head), :], by_rows, preferred_element_type=jnp.float32
+        ).astype(low)
+        g_own[head] = grads.reshape(2, block_rows, dim)
+        product = grads.astype(jnp.float32) * a_own[:, head_cut(head)].astype(jnp.float32)
+        deltas = lax.dot_general(
+            jnp.ones((stat_rows[0], dim), jnp.float32), product, by_rows,
+            precision=lax.Precision.HIGHEST, preferred_element_type=jnp.float32,
+        )
+        logs = jnp.broadcast_to(l_own[pl.ds(head, 1), :], stat_rows)
+        stats = jnp.where(log_row, logs, deltas)
+        turned = pltpu.roll(stats, block_rows, 1)
+        s_own[head, 0] = jnp.where(early_half, stats, turned)
+        s_own[head, 1] = jnp.where(early_half, turned, stats)
+
+        @pl.when(step > 1)
+        def _():
+            before = lax.rem(me + step - 1, count)
+            for copy in head_copies(grad_pieces(before, me), 3, step - 1, me, (before, core)):
+                copy.start()
+
+    g_all[owner_blocks(me)] = g_own[me]
+    s_all[owner_blocks(me)] = s_own[me]
+
+    for copy in owns:
+        copy.wait()
+
+    @pl.loop(1, members)
+    def _(step):
+        slot, to_column, to_core = plane_peer(step)
+        device = (plane + to_column, to_core)
+        for copy in plane_copies(to_column, to_core, own_slot, step, own_slot, device):
+            copy.wait_send()
+        for copy in plane_copies(column, core, slot, step, slot, device):
+            copy.wait_recv()
+
+    rows_all = members * a_all.shape[1]
+    grads_in = b_all[...].reshape(rows_all, half)
+    for part in range(side):
+        saved = a_all[:, :, pl.ds(part * dim, dim)].reshape(rows_all, dim)
+        w_part[part] = lax.dot_general(
+            saved, grads_in, by_columns, preferred_element_type=jnp.float32
+        ).astype(low)
+    w_line[row] = w_part[row]
+    for step in range(1, side):
+        to_row = lax.rem(row + step, side)
+        line_copy(to_row, row, step, row, (to_row * side + column, core)).start()
+
+    @pl.loop(1, count)
+    def _(step):
+        peer = lax.rem(me + step, count)
+        device = (peer, core)
+        for copy in head_copies(row_pieces(peer, me), 0, step, me, device):
+            copy.wait_send()
+        for copy in head_copies(grad_pieces(peer, me), 3, step, me, device):
+            copy.wait_send()
+        for copy in head_copies(row_pieces(me, peer), 0, step, peer, device):
+            copy.wait_recv()
+        for copy in head_copies(grad_pieces(me, peer), 3, step, peer, device):
+            copy.wait_recv()
+
+    blocks = places.shape[0] // 2
+    length = count * rows
+    for place in range(blocks):
+        block = places[place]
+        target = pl.ds(place * block_rows, block_rows)
+        for raw, ordered in ((q_all, q_row), (k_all, k_row), (v_all, v_row), (g_all, g_row)):
+            ordered[target, :] = raw[block]
+    for pair_at in range(blocks // 2):
+        early = s_all[places[2 * pair_at]]
+        late = s_all[places[2 * pair_at + 1]]
+        s_row[pair_at] = jnp.where(early_half, early, late)
+    tiles = length // tile
+    per_tile = tile // rows
+    tile_blocks = tile // block_rows
+    dq[...] = jnp.zeros_like(dq)
+
+    def pair(i, j, diagonal, sums):
+        key_cut = pl.ds(j * tile, tile)
+        query_cut = pl.ds(pl.multiple_of(i * tile, tile), tile)
+        k_tile, v_tile = k_row[key_cut, :], v_row[key_cut, :]
+        q_tile, g_tile = q_row[query_cut, :], g_row[query_cut, :]
+        log_line = jnp.concatenate(
+            [s_row[i * per_tile + m, 0:1, :] for m in range(per_tile)], axis=1
+        )
+        delta_line = jnp.concatenate(
+            [s_row[i * per_tile + m, 1:2, :] for m in range(per_tile)], axis=1
+        )
+        scores = lax.dot_general(k_tile, q_tile, by_rows, preferred_element_type=jnp.float32)
+        probs = jnp.exp(scores * scaling - log_line)
+        if diagonal:
+            key_at = lax.broadcasted_iota(jnp.int32, (tile, tile), 0)
+            query_at = lax.broadcasted_iota(jnp.int32, (tile, tile), 1)
+            probs = jnp.where(key_at <= query_at, probs, 0.0)
+        dprobs = lax.dot_general(v_tile, g_tile, by_rows, preferred_element_type=jnp.float32)
+        dscores = (probs * (dprobs - delta_line)).astype(low)
+        dv_sum = sums[1] + jnp.dot(
+            probs.astype(low), g_tile, preferred_element_type=jnp.float32
+        )
+        dk_sum = sums[0] + jnp.dot(dscores, q_tile, preferred_element_type=jnp.float32)
+        dq[pl.ds(i * tile_blocks, tile_blocks)] += lax.dot_general(
+            dscores, k_tile, by_columns, preferred_element_type=jnp.float32
+        ).reshape(tile_blocks, block_rows, dim)
+        return dk_sum, dv_sum
+
+    for j in range(tiles):
+        zero = jnp.zeros((tile, dim), jnp.float32)
+        sums = pair(j, j, True, (zero, zero))
+        if j + 1 < tiles:
+            sums = lax.fori_loop(
+                j + 1, tiles, lambda i, carry: pair(i, j, False, carry), sums
+            )
+        key_blocks = pl.ds(j * tile_blocks, tile_blocks)
+        dk[key_blocks] = sums[0].reshape(tile_blocks, block_rows, dim)
+        dv[key_blocks] = sums[1].reshape(tile_blocks, block_rows, dim)
+    for block in range(blocks):
+        place = places[blocks + block]
+        target = pl.ds(block % 2 * block_rows, block_rows)
+        q_back[block // 2, target, :] = (dq[place] * scaling).astype(low)
+        k_back[block // 2, target, :] = (dk[place] * scaling).astype(low)
+        v_back[block // 2, target, :] = dv[place].astype(low)
+
+    @pl.loop(1, count)
+    def _(step):
+        peer = lax.rem(me + step, count)
+        for copy in back_copies(peer, me, step, me, (peer, core)):
+            copy.start()
+
+    returns = [
+        pltpu.make_async_copy(source, target, local.at[at])
+        for at, (source, target) in enumerate(back_pieces(me, me))
+    ]
+    for copy in returns:
+        copy.start()
+
+    for step in range(1, side):
+        to_row = lax.rem(row + step, side)
+        device = (to_row * side + column, core)
+        line_copy(to_row, row, step, row, device).wait_send()
+        line_copy(row, to_row, step, to_row, device).wait_recv()
+    total = w_line[0].astype(jnp.float32)
+    for part in range(1, side):
+        total = total + w_line[part].astype(jnp.float32)
+    w_half[core] = total.astype(low)
+
+    def half_copy(slot, turn, other):
+        return remote(
+            w_half.at[slot], w_half.at[slot], half_send.at[turn], half_recv.at[slot], (me, other)
+        )
+
+    for turn in range(1, cores):
+        half_copy(core, turn, lax.rem(core + turn, cores)).start()
+    for turn in range(1, cores):
+        other = lax.rem(core + turn, cores)
+        half_copy(core, turn, other).wait_send()
+        half_copy(other, turn, other).wait_recv()
+    for slot in range(cores):
+        w_out[:, pl.ds(slot * half, half)] = w_half[slot].astype(jnp.float32)
+
+    for copy in returns:
+        copy.wait()
+
+    @pl.loop(1, count)
+    def _(step):
+        peer = lax.rem(me + step, count)
+        for copy in back_copies(peer, me, step, me, (peer, core)):
+            copy.wait_send()
+        for copy in back_copies(me, peer, step, peer, (peer, core)):
+            copy.wait_recv()
+
+
+def head_per_device(
+    side, cores, block_pos, queries, keys, values, attn_out, log_sums, grad_out, out_weight
+):
+    count = lax.axis_size("seq")
+    rows = queries.shape[1]
+    width = queries.shape[2]
+    heads = log_sums.shape[1]
+    dim = width // heads
+    scaling = dim ** (-0.5)
+    out_width = grad_out.shape[2]
+    share = out_width // cores
+    length = count * rows
+    low = jnp.bfloat16
+    table = block_pos[0]
+    numbers = jnp.arange(table.shape[0], dtype=jnp.int32)
+    inverse = jnp.sum(
+        jnp.where(table[None, :] == numbers[:, None], numbers[None, :], 0), axis=1
+    )
+    block_rows = rows // 2
+    places = jnp.concatenate([inverse, table])
+    dma = pltpu.SemaphoreType.DMA
+    members = side * cores
+    tile = min(512, length)
+    vmem = pl.BlockSpec(memory_space=pltpu.VMEM)
+    wide = (length, dim)
+    block_shape = (2 * count, block_rows, dim)
+    split = (count, rows, dim)
+    stat = (count, 8, rows)
+    grad_queries, grad_keys, grad_values, weight_share = pl.pallas_call(
+        functools.partial(fused_kernel, count, side, cores, dim, tile, scaling),
+        out_shape=[jax.ShapeDtypeStruct((rows, width), low)] * 3
+        + [jax.ShapeDtypeStruct((dim, out_width), jnp.float32)],
+        in_specs=[pl.BlockSpec(memory_space=pltpu.SMEM)] + [ANY] * 7,
+        out_specs=[ANY] * 3 + [vmem],
+        scratch_shapes=[pltpu.VMEM(block_shape, low)] * 4
+        + [
+            pltpu.VMEM((2 * count, 8, rows), jnp.float32),
+            pltpu.VMEM((members, rows, side * dim), low),
+            pltpu.VMEM((members, rows, share), low),
+            pltpu.VMEM((rows, width), low),
+            pltpu.VMEM((rows, out_width), low),
+            pltpu.VMEM((heads, rows), jnp.float32),
+            pltpu.VMEM(out_weight.shape, low),
+            pltpu.VMEM((count, 2, block_rows, dim), low),
+            pltpu.VMEM((count, 2, 8, rows), jnp.float32),
+        ]
+        + [pltpu.VMEM(wide, low)] * 4
+        + [pltpu.VMEM(stat, jnp.float32)]
+        + [pltpu.VMEM(block_shape, jnp.float32)] * 3
+        + [pltpu.VMEM(split, low)] * 3
+        + [pltpu.VMEM((side, dim, share), low)] * 2
+        + [pltpu.VMEM((cores, dim, share), low)]
+        + [
+            dma((5, count)), dma((5, count)),
+            dma((side + 1, members)), dma((side + 1, members)),
+            dma((side,)), dma((side,)),
+            dma((3, count)), dma((3, count)),
+            dma((cores,)), dma((cores,)), dma((side + 8,)),
+        ],
+        compiler_params=pltpu.CompilerParams(
+            collective_id=0, has_side_effects=True, vmem_limit_bytes=60 * 1024 * 1024
+        ),
+    )(
+        places,
+        *(part.reshape(2, block_rows, width) for part in (queries, keys, values)),
+        attn_out[0], grad_out[0], log_sums[0],
+        out_weight,
+    )
+    return grad_queries[None], grad_keys[None], grad_values[None], weight_share
+
+
+def make_per_device(mesh):
+    count = mesh.shape["seq"]
+    cores = mesh.shape["dp"]
+    side = int(round(count ** 0.5))
+
+    def per_device(block_pos, queries, keys, values, attn_out, log_sums, grad_out, out_weight):
+        heads = log_sums.shape[1]
+        arguments = (
+            block_pos, queries, keys, values, attn_out, log_sums, grad_out, out_weight
+        )
+        if heads == count and side * side == count:
+            return head_per_device(side, cores, *arguments)
+        return grid_per_device(*arguments)
+
+    return per_device
+
+
 def solution(mesh):
     in_specs = (
         P("dp", None),
@@ -172,5 +592,5 @@
     )
     out_specs = (P("dp", "seq", None), P("dp", "seq", None), P("dp", "seq", None), P("seq", None))
     return jax.shard_map(
-        per_device, mesh=mesh, in_specs=in_specs, out_specs=out_specs, check_vma=False
-    )
+        make_per_device(mesh), mesh=mesh, in_specs=in_specs, out_specs=out_specs, check_vma=False
+    )

time: 442 us -> 140 us (0.32)
  the two profiles are of different devices: /device:TPU:3 before, /device:TPU:15 now
where the time goes in v2:
time: 140 us; the launch traced here: 138 us
  Pallas kernels  128 us (91%)
  local copies, waits for them, and re-layouts  7.94 us (6%)
  other arithmetic  2.01 us (1%)
    pallas_call x1, Pallas kernels, head_per_device(): pl.pallas_call(functools.partial(fused_kernel, count, side, cores, dim, t...  128 us
    unnamed x4, local copies, waits for them, and re-layouts  7.94 us

profile of v2, /device:TPU:15, one launch (start us, length us, event | category | flops | bytes accessed | tf_op | source)
XLA Modules:
  0.0 138.4 jit_solution(12392378154138627605)
XLA Ops:
  0.6 0.8 select_reduce_fusion
  1.4 1.2 pad_add_fusion.places
  2.6 127.8 %shard_map.111 = (bf16[128,2048]{1,0:T(8,128)(2,1)}, bf16[128,2048]{1,0:T(8,128)(2,1)}, bf16[128,2048]{1,0:T(8,128)(2,1)}, f32[128,2048]{1,0:T(8,128)}) custom-call(s32[64]{0:T(128)} %pad_add_fusion.places, bf16[2,64,2048]{2,1,0:T(8,128)(2,1)} %bitcast.10, bf16[2,64,2048]{2,1,0:T(8,128)(2,1)} %bitcast.11, bf16[2,64,2048]{2,1,0:T(8,128)(2,1)} %bitcast.12, ...), custom_call_target="tpu_custom_call" | custom-call | tf_op jit(solution)/shard_map/pallas_call | solution.py:522
  130.4 1.9 %copy.16 = bf16[1,128,2048]{2,1,0:T(8,128)(2,1)} copy(bf16[1,128,2048]{2,1,0:T(8,128)(2,1)} %bitcast.17) | data formatting | bytes 1048576
  132.3 1.9 %copy.17 = bf16[1,128,2048]{2,1,0:T(8,128)(2,1)} copy(bf16[1,128,2048]{2,1,0:T(8,128)(2,1)} %bitcast.16) | data formatting | bytes 1048576
  134.2 1.9 %copy.18 = bf16[1,128,2048]{2,1,0:T(8,128)(2,1)} copy(bf16[1,128,2048]{2,1,0:T(8,128)(2,1)} %bitcast.15) | data formatting | bytes 1048576
  136.1 2.3 %copy.19 = f32[128,2048]{1,0:T(8,128)} copy(f32[128,2048]{1,0:T(8,128)} %get-tuple-element.19) | data formatting | bytes 2097152

commit v3 on v2

--- a/solution.py
+++ b/solution.py
@@ -167,41 +167,37 @@
 ANY = pl.BlockSpec(memory_space=pl.ANY)
 
 
-def enter(count, side, cores, me, core):
+def enter(count, cores, me, core):
     barrier = pltpu.get_barrier_semaphore()
-    plane = me // side * side
     for step in range(1, count):
         pl.semaphore_signal(
             barrier, inc=1, device_id=(lax.rem(me + step, count), core), device_id_type=MESH
         )
     total = count - 1
     for turn in range(1, cores):
-        for step in range(side):
-            peer = (plane + step, lax.rem(core + turn, cores))
-            pl.semaphore_signal(barrier, inc=1, device_id=peer, device_id_type=MESH)
-            total += 1
+        peer = (me, lax.rem(core + turn, cores))
+        pl.semaphore_signal(barrier, inc=1, device_id=peer, device_id_type=MESH)
+        total += 1
     pl.semaphore_wait(barrier, total)
 
 
 def fused_kernel(
     count, side, cores, dim, tile, scaling,
-    places, q_in, k_in, v_in, a_in, b_in, l_in, w_in,
+    sources, places, q_in, k_in, v_in, a_in, b_in, l_in, w_in,
     q_out, k_out, v_out, w_out,
     q_all, k_all, v_all, g_all, s_all, a_all, b_all,
     a_own, b_own, l_own, w_own, g_own, s_own,
     q_row, k_row, v_row, g_row, s_row, dq, dk, dv,
-    q_back, k_back, v_back, w_part, w_line, w_half,
+    q_back, k_back, v_back, w_part, w_line, w_half, w_core, w_land,
     send, recv, plane_send, plane_recv, line_send, line_recv,
-    back_send, back_recv, half_send, half_recv, local,
+    back_send, back_recv, half_send, half_recv, core_send, core_recv, local,
 ):
     me = lax.axis_index("seq")
     core = lax.axis_index("dp")
     column = lax.rem(me, side)
     plane = me - column
     row = me // side
-    half = b_all.shape[2]
-    members = side * cores
-    own_slot = column * cores + core
+    half = w_half.shape[2]
     low = jnp.bfloat16
 
     loads = [
@@ -212,7 +208,7 @@
     ]
     for copy in loads:
         copy.start()
-    enter(count, side, cores, me, core)
+    enter(count, cores, me, core)
 
     def head_cut(head):
         return pl.ds(pl.multiple_of(head * dim, dim), dim)
@@ -247,23 +243,31 @@
             for at, (source, target) in enumerate(pieces)
         ]
 
-    def plane_pieces(to_column, to_core, slot):
+    def plane_pieces(to_column, slot):
         pairs = []
         for part in range(side):
             cut = head_cut(part * side + to_column)
             pairs.append((a_in.at[:, cut], a_all.at[slot, :, pl.ds(part * dim, dim)]))
-        cut = pl.ds(pl.multiple_of(to_core * half, half), half)
-        return pairs + [(b_in.at[:, cut], b_all.at[slot])]
-
-    def plane_copies(to_column, to_core, slot, out_index, in_index, device):
+        return pairs + [(b_in, b_all.at[slot])]
+
+    def plane_copies(to_column, slot, out_index, in_index, device):
         return [
             remote(source, target, plane_send.at[at, out_index], plane_recv.at[at, in_index], device)
-            for at, (source, target) in enumerate(plane_pieces(to_column, to_core, slot))
+            for at, (source, target) in enumerate(plane_pieces(to_column, slot))
         ]
 
     def plane_peer(step):
-        slot = lax.rem(own_slot + step, members)
-        return slot, slot // cores, lax.rem(slot, cores)
+        return lax.rem(column + step, side)
+
+    def far_first(turn):
+        far = count - side
+        return jnp.where(turn < far, turn + side, lax.rem(turn - far + 1, side))
+
+    def core_copy(to_core, slot, turn):
+        return remote(
+            w_core.at[to_core], w_land.at[slot], core_send.at[turn], core_recv.at[slot],
+            (me, to_core),
+        )
 
     def line_copy(to_row, slot, out_index, in_index, device):
         return remote(
@@ -284,24 +288,17 @@
             for at, (source, target) in enumerate(back_pieces(owner, head))
         ]
 
-    @pl.loop(1, count)
-    def _(step):
+    @pl.loop(0, count - 1)
+    def _(turn):
+        step = far_first(turn)
         peer = lax.rem(me + step, count)
         for copy in head_copies(row_pieces(peer, me), 0, step, me, (peer, core)):
             copy.start()
 
-    @pl.loop(1, members)
-    def _(step):
-        slot, to_column, to_core = plane_peer(step)
-        for copy in plane_copies(
-            to_column, to_core, own_slot, step, own_slot, (plane + to_column, to_core)
-        ):
-            copy.start()
-
     owns = [
         pltpu.make_async_copy(source, target, local.at[4 + at])
         for at, (source, target) in enumerate(
-            row_pieces(me, me) + plane_pieces(column, core, own_slot)
+            row_pieces(me, me) + plane_pieces(column, column)
         )
     ]
     for copy in owns:
@@ -317,9 +314,9 @@
     early_half = lax.broadcasted_iota(jnp.int32, stat_rows, 1) < block_rows
     log_row = stat_at < 1
 
-    @pl.loop(1, count + 1)
-    def _(step):
-        head = lax.rem(me + step, count)
+    @pl.loop(0, count)
+    def _(turn):
+        head = lax.rem(me + far_first(turn), count)
         grads = lax.dot_general(
             b_own[...], w_own[head_cut(head), :], by_rows, preferred_element_type=jnp.float32
         ).astype(low)
@@ -335,11 +332,17 @@
         s_own[head, 0] = jnp.where(early_half, stats, turned)
         s_own[head, 1] = jnp.where(early_half, turned, stats)
 
-        @pl.when(step > 1)
+        @pl.when(turn > 0)
         def _():
-            before = lax.rem(me + step - 1, count)
-            for copy in head_copies(grad_pieces(before, me), 3, step - 1, me, (before, core)):
+            step = far_first(turn - 1)
+            before = lax.rem(me + step, count)
+            for copy in head_copies(grad_pieces(before, me), 3, step, me, (before, core)):
                 copy.start()
+
+    for step in range(1, side):
+        to_column = plane_peer(step)
+        for copy in plane_copies(to_column, column, step, column, (plane + to_column, core)):
+            copy.start()
 
     g_all[owner_blocks(me)] = g_own[me]
     s_all[owner_blocks(me)] = s_own[me]
@@ -347,22 +350,34 @@
     for copy in owns:
         copy.wait()
 
-    @pl.loop(1, members)
-    def _(step):
-        slot, to_column, to_core = plane_peer(step)
-        device = (plane + to_column, to_core)
-        for copy in plane_copies(to_column, to_core, own_slot, step, own_slot, device):
+    for step in range(1, side):
+        to_column = plane_peer(step)
+        device = (plane + to_column, core)
+        for copy in plane_copies(to_column, column, step, column, device):
             copy.wait_send()
-        for copy in plane_copies(column, core, slot, step, slot, device):
+        for copy in plane_copies(column, to_column, step, to_column, device):
             copy.wait_recv()
 
-    rows_all = members * a_all.shape[1]
-    grads_in = b_all[...].reshape(rows_all, half)
+    rows_all = side * rows
+    for to_core in range(cores):
+        grads_in = b_all[:, :, pl.ds(to_core * half, half)].reshape(rows_all, half)
+        for part in range(side):
+            saved = a_all[:, :, pl.ds(part * dim, dim)].reshape(rows_all, dim)
+            w_core[to_core, part] = lax.dot_general(
+                saved, grads_in, by_columns, preferred_element_type=jnp.float32
+            ).astype(low)
+    for turn in range(1, cores):
+        core_copy(lax.rem(core + turn, cores), core, turn).start()
+    w_land[core] = w_core[core]
+    for turn in range(1, cores):
+        other = lax.rem(core + turn, cores)
+        core_copy(other, core, turn).wait_send()
+        core_copy(core, other, turn).wait_recv()
     for part in range(side):
-        saved = a_all[:, :, pl.ds(part * dim, dim)].reshape(rows_all, dim)
-        w_part[part] = lax.dot_general(
-            saved, grads_in, by_columns, preferred_element_type=jnp.float32
-        ).astype(low)
+        merged = w_land[0, part].astype(jnp.float32)
+        for slot in range(1, cores):
+            merged = merged + w_land[slot, part].astype(jnp.float32)
+        w_part[part] = merged.astype(low)
     w_line[row] = w_part[row]
     for step in range(1, side):
         to_row = lax.rem(row + step, side)
@@ -381,16 +396,16 @@
         for copy in head_copies(grad_pieces(me, peer), 3, step, peer, device):
             copy.wait_recv()
 
-    blocks = places.shape[0] // 2
+    blocks = places.shape[0]
     length = count * rows
     for place in range(blocks):
-        block = places[place]
+        block = sources[place]
         target = pl.ds(place * block_rows, block_rows)
         for raw, ordered in ((q_all, q_row), (k_all, k_row), (v_all, v_row), (g_all, g_row)):
             ordered[target, :] = raw[block]
     for pair_at in range(blocks // 2):
-        early = s_all[places[2 * pair_at]]
-        late = s_all[places[2 * pair_at + 1]]
+        early = s_all[sources[2 * pair_at]]
+        late = s_all[sources[2 * pair_at + 1]]
         s_row[pair_at] = jnp.where(early_half, early, late)
     tiles = length // tile
     per_tile = tile // rows
@@ -436,14 +451,15 @@
         dk[key_blocks] = sums[0].reshape(tile_blocks, block_rows, dim)
         dv[key_blocks] = sums[1].reshape(tile_blocks, block_rows, dim)
     for block in range(blocks):
-        place = places[blocks + block]
+        place = places[block]
         target = pl.ds(block % 2 * block_rows, block_rows)
         q_back[block // 2, target, :] = (dq[place] * scaling).astype(low)
         k_back[block // 2, target, :] = (dk[place] * scaling).astype(low)
         v_back[block // 2, target, :] = dv[place].astype(low)
 
-    @pl.loop(1, count)
-    def _(step):
+    @pl.loop(0, count - 1)
+    def _(turn):
+        step = far_first(turn)
         peer = lax.rem(me + step, count)
         for copy in back_copies(peer, me, step, me, (peer, core)):
             copy.start()
@@ -477,7 +493,7 @@
         half_copy(core, turn, other).wait_send()
         half_copy(other, turn, other).wait_recv()
     for slot in range(cores):
-        w_out[:, pl.ds(slot * half, half)] = w_half[slot].astype(jnp.float32)
+        w_out[:, pl.ds(slot * half, half)] = w_half[slot]
 
     for copy in returns:
         copy.wait()
@@ -510,9 +526,7 @@
         jnp.where(table[None, :] == numbers[:, None], numbers[None, :], 0), axis=1
     )
     block_rows = rows // 2
-    places = jnp.concatenate([inverse, table])
     dma = pltpu.SemaphoreType.DMA
-    members = side * cores
     tile = min(512, length)
     vmem = pl.BlockSpec(memory_space=pltpu.VMEM)
     wide = (length, dim)
@@ -522,14 +536,14 @@
     grad_queries, grad_keys, grad_values, weight_share = pl.pallas_call(
         functools.partial(fused_kernel, count, side, cores, dim, tile, scaling),
         out_shape=[jax.ShapeDtypeStruct((rows, width), low)] * 3
-        + [jax.ShapeDtypeStruct((dim, out_width), jnp.float32)],
-        in_specs=[pl.BlockSpec(memory_space=pltpu.SMEM)] + [ANY] * 7,
+        + [jax.ShapeDtypeStruct((dim, out_width), low)],
+        in_specs=[pl.BlockSpec(memory_space=pltpu.SMEM)] * 2 + [ANY] * 7,
         out_specs=[ANY] * 3 + [vmem],
         scratch_shapes=[pltpu.VMEM(block_shape, low)] * 4
         + [
             pltpu.VMEM((2 * count, 8, rows), jnp.float32),
-            pltpu.VMEM((members, rows, side * dim), low),
-            pltpu.VMEM((members, rows, share), low),
+            pltpu.VMEM((side, rows, side * dim), low),
+            pltpu.VMEM((side, rows, out_width), low),
             pltpu.VMEM((rows, width), low),
             pltpu.VMEM((rows, out_width), low),
             pltpu.VMEM((heads, rows), jnp.float32),
@@ -543,23 +557,36 @@
         + [pltpu.VMEM(split, low)] * 3
         + [pltpu.VMEM((side, dim, share), low)] * 2
         + [pltpu.VMEM((cores, dim, share), low)]
+        + [pltpu.VMEM((cores, side, dim, share), low)] * 2
         + [
             dma((5, count)), dma((5, count)),
-            dma((side + 1, members)), dma((side + 1, members)),
+            dma((side + 1, side)), dma((side + 1, side)),
             dma((side,)), dma((side,)),
             dma((3, count)), dma((3, count)),
-            dma((cores,)), dma((cores,)), dma((side + 8,)),
+            dma((cores,)), dma((cores,)), dma((cores,)), dma((cores,)), dma((side + 8,)),
         ],
         compiler_params=pltpu.CompilerParams(
             collective_id=0, has_side_effects=True, vmem_limit_bytes=60 * 1024 * 1024
         ),
     )(
-        places,
+        inverse, table,
         *(part.reshape(2, block_rows, width) for part in (queries, keys, values)),
         attn_out[0], grad_out[0], log_sums[0],
         out_weight,
     )
+    grad_queries, grad_keys, grad_values, weight_share = pl.pallas_call(
+        leave_kernel,
+        out_shape=[jax.ShapeDtypeStruct((rows, width), low)] * 3
+        + [jax.ShapeDtypeStruct((dim, out_width), jnp.float32)],
+        in_specs=[vmem] * 4,
+        out_specs=[vmem] * 4,
+    )(grad_queries, grad_keys, grad_values, weight_share)
     return grad_queries[None], grad_keys[None], grad_values[None], weight_share
+
+
+def leave_kernel(q_in, k_in, v_in, w_in, q_out, k_out, v_out, w_out):
+    for source, target in ((q_in, q_out), (k_in, k_out), (v_in, v_out), (w_in, w_out)):
+        target[...] = source[...].astype(target.dtype)
 
 
 def make_per_device(mesh):

time: 140 us -> 136 us (0.971); the launches traced: 138 us -> 136 us
  local copies, waits for them, and re-layouts: 7.94 us -> 0 us
  Pallas kernels: 128 us -> 134 us
    unnamed x4 -> x0, local copies, waits for them, and re-layouts: 7.94 us -> none
    pallas_call x1, Pallas kernels: 128 us -> 131 us  [head_per_device(): pl.pallas_call(functools.partial(fused_kernel, count, side, cores, dim, t...]
    pallas_call x0 -> x1, Pallas kernels: none -> 3.04 us  [head_per_device(): pl.pallas_call(leave_kernel, out_shape=[jax.ShapeDtypeStruct((rows, width...]
where the time goes in v3:
time: 136 us
  Pallas kernels  134 us (99%)
    pallas_call x1, Pallas kernels, head_per_device(): pl.pallas_call(functools.partial(fused_kernel, count, side, cores, dim, t...  131 us
    pallas_call x1, Pallas kernels, head_per_device(): pl.pallas_call(leave_kernel, out_shape=[jax.ShapeDtypeStruct((rows, width...  3.04 us

profile of v3, /device:TPU:15, one launch (start us, length us, event | category | flops | bytes accessed | tf_op | source)
XLA Modules:
  0.0 135.9 jit_solution(1505966342428596584)
XLA Ops:
  0.6 1.3 select_reduce_fusion.sources
  1.9 131.0 %shard_map.111 = (bf16[128,2048]{1,0:T(8,128)(2,1)}, bf16[128,2048]{1,0:T(8,128)(2,1)}, bf16[128,2048]{1,0:T(8,128)(2,1)}, bf16[128,2048]{1,0:T(8,128)(2,1)}) custom-call(s32[32]{0:T(128)} %select_reduce_fusion.sources, s32[32]{0:T(128)} %bitcast.17, bf16[2,64,2048]{2,1,0:T(8,128)(2,1)} %bitcast.10, bf16[2,64,2048]{2,1,0:T(8,128)(2,1)} %bitcast.11, ...), custom_call_target="tpu_custom_call" | custom-call | tf_op jit(solution)/shard_map/pallas_call | solution.py:536
  132.9 3.0 %shard_map.112 = (bf16[128,2048]{1,0:T(8,128)(2,1)}, bf16[128,2048]{1,0:T(8,128)(2,1)}, bf16[128,2048]{1,0:T(8,128)(2,1)}, f32[128,2048]{1,0:T(8,128)}) custom-call(bf16[128,2048]{1,0:T(8,128)(2,1)} %get-tuple-element.12.q_in, bf16[128,2048]{1,0:T(8,128)(2,1)} %get-tuple-element.13.k_in, bf16[128,2048]{1,0:T(8,128)(2,1)} %get-tuple-element.14.v_in, ...), custom_call_target="tpu_custom_call" | custom-call | tf_op jit(solution)/shard_map/pallas_call | solution.py:577

commit v4 on v3

--- a/solution.py
+++ b/solution.py
@@ -198,6 +198,7 @@
     plane = me - column
     row = me // side
     half = w_half.shape[2]
+    groups, _, _, _, sub = w_core.shape
     low = jnp.bfloat16
 
     loads = [
@@ -248,7 +249,15 @@
         for part in range(side):
             cut = head_cut(part * side + to_column)
             pairs.append((a_in.at[:, cut], a_all.at[slot, :, pl.ds(part * dim, dim)]))
-        return pairs + [(b_in, b_all.at[slot])]
+        for group in range(groups):
+            for to_core in range(cores):
+                cut = pl.ds(to_core * half + group * sub, sub)
+                pairs.append((b_in.at[:, cut], b_all.at[slot, :, cut]))
+        return pairs
+
+    def group_of(copies, group):
+        first = side + group * cores if group else 0
+        return copies[first : side + (group + 1) * cores]
 
     def plane_copies(to_column, slot, out_index, in_index, device):
         return [
@@ -263,16 +272,16 @@
         far = count - side
         return jnp.where(turn < far, turn + side, lax.rem(turn - far + 1, side))
 
-    def core_copy(to_core, slot, turn):
+    def core_copy(group, to_core, slot, turn):
         return remote(
-            w_core.at[to_core], w_land.at[slot], core_send.at[turn], core_recv.at[slot],
-            (me, to_core),
-        )
-
-    def line_copy(to_row, slot, out_index, in_index, device):
+            w_core.at[group, to_core], w_land.at[group, slot], core_send.at[group, turn],
+            core_recv.at[group, slot], (me, to_core),
+        )
+
+    def line_copy(group, to_row, slot, out_index, in_index, device):
         return remote(
-            w_part.at[to_row], w_line.at[slot], line_send.at[out_index],
-            line_recv.at[in_index], device,
+            w_part.at[group, to_row], w_line.at[group, slot], line_send.at[group, out_index],
+            line_recv.at[group, in_index], device,
         )
 
     def back_pieces(owner, head):
@@ -339,10 +348,14 @@
             for copy in head_copies(grad_pieces(before, me), 3, step, me, (before, core)):
                 copy.start()
 
-    for step in range(1, side):
-        to_column = plane_peer(step)
-        for copy in plane_copies(to_column, column, step, column, (plane + to_column, core)):
-            copy.start()
+    for group in range(groups):
+        for step in range(1, side):
+            to_column = plane_peer(step)
+            device = (plane + to_column, core)
+            for copy in group_of(
+                plane_copies(to_column, column, step, column, device), group
+            ):
+                copy.start()
 
     g_all[owner_blocks(me)] = g_own[me]
     s_all[owner_blocks(me)] = s_own[me]
@@ -350,38 +363,55 @@
     for copy in owns:
         copy.wait()
 
+    rows_all = side * rows
+
+    def weight_part(part, grads_in):
+        saved = a_all[:, :, pl.ds(part * dim, dim)].reshape(rows_all, dim)
+        return lax.dot_general(
+            saved, grads_in, by_columns, preferred_element_type=jnp.float32
+        ).astype(low)
+
+    def group_grads(to_core, group):
+        cut = pl.ds(pl.multiple_of(to_core * half + group * sub, sub), sub)
+        return b_all[:, :, cut].reshape(rows_all, sub)
+
+    for group in range(groups):
+        for step in range(1, side):
+            to_column = plane_peer(step)
+            device = (plane + to_column, core)
+            for copy in group_of(
+                plane_copies(column, to_column, step, to_column, device), group
+            ):
+                copy.wait_recv()
+        for turn in range(1, cores):
+            to_core = lax.rem(core + turn, cores)
+            grads_in = group_grads(to_core, group)
+            for part in range(side):
+                w_core[group, to_core, part] = weight_part(part, grads_in)
+            core_copy(group, to_core, core, turn).start()
+        grads_in = group_grads(core, group)
+        for part in range(side):
+            w_land[group, core, part] = weight_part(part, grads_in)
+        for turn in range(1, cores):
+            other = lax.rem(core + turn, cores)
+            core_copy(group, other, core, turn).wait_send()
+            core_copy(group, core, other, turn).wait_recv()
+        for part in range(side):
+            merged = w_land[group, 0, part].astype(jnp.float32)
+            for slot in range(1, cores):
+                merged = merged + w_land[group, slot, part].astype(jnp.float32)
+            w_part[group, part] = merged.astype(low)
+        w_line[group, row] = w_part[group, row]
+        for step in range(1, side):
+            to_row = lax.rem(row + step, side)
+            line_copy(
+                group, to_row, row, step, row, (to_row * side + column, core)
+            ).start()
     for step in range(1, side):
         to_column = plane_peer(step)
         device = (plane + to_column, core)
         for copy in plane_copies(to_column, column, step, column, device):
             copy.wait_send()
-        for copy in plane_copies(column, to_column, step, to_column, device):
-            copy.wait_recv()
-
-    rows_all = side * rows
-    for to_core in range(cores):
-        grads_in = b_all[:, :, pl.ds(to_core * half, half)].reshape(rows_all, half)
-        for part in range(side):
-            saved = a_all[:, :, pl.ds(part * dim, dim)].reshape(rows_all, dim)
-            w_core[to_core, part] = lax.dot_general(
-                saved, grads_in, by_columns, preferred_element_type=jnp.float32
-            ).astype(low)
-    for turn in range(1, cores):
-        core_copy(lax.rem(core + turn, cores), core, turn).start()
-    w_land[core] = w_core[core]
-    for turn in range(1, cores):
-        other = lax.rem(core + turn, cores)
-        core_copy(other, core, turn).wait_send()
-        core_copy(core, other, turn).wait_recv()
-    for part in range(side):
-        merged = w_land[0, part].astype(jnp.float32)
-        for slot in range(1, cores):
-            merged = merged + w_land[slot, part].astype(jnp.float32)
-        w_part[part] = merged.astype(low)
-    w_line[row] = w_part[row]
-    for step in range(1, side):
-        to_row = lax.rem(row + step, side)
-        line_copy(to_row, row, step, row, (to_row * side + column, core)).start()
 
     @pl.loop(1, count)
     def _(step):
@@ -471,15 +501,16 @@
     for copy in returns:
         copy.start()
 
-    for step in range(1, side):
-        to_row = lax.rem(row + step, side)
-        device = (to_row * side + column, core)
-        line_copy(to_row, row, step, row, device).wait_send()
-        line_copy(row, to_row, step, to_row, device).wait_recv()
-    total = w_line[0].astype(jnp.float32)
-    for part in range(1, side):
-        total = total + w_line[part].astype(jnp.float32)
-    w_half[core] = total.astype(low)
+    for group in range(groups):
+        for step in range(1, side):
+            to_row = lax.rem(row + step, side)
+            device = (to_row * side + column, core)
+            line_copy(group, to_row, row, step, row, device).wait_send()
+            line_copy(group, row, to_row, step, to_row, device).wait_recv()
+        total = w_line[group, 0].astype(jnp.float32)
+        for part in range(1, side):
+            total = total + w_line[group, part].astype(jnp.float32)
+        w_half[core, :, pl.ds(group * sub, sub)] = total.astype(low)
 
     def half_copy(slot, turn, other):
         return remote(
@@ -526,6 +557,9 @@
         jnp.where(table[None, :] == numbers[:, None], numbers[None, :], 0), axis=1
     )
     block_rows = rows // 2
+    groups = 2
+    sub = share // groups
+    pieces = side + groups * cores
     dma = pltpu.SemaphoreType.DMA
     tile = min(512, length)
     vmem = pl.BlockSpec(memory_space=pltpu.VMEM)
@@ -555,15 +589,16 @@
         + [pltpu.VMEM(stat, jnp.float32)]
         + [pltpu.VMEM(block_shape, jnp.float32)] * 3
         + [pltpu.VMEM(split, low)] * 3
-        + [pltpu.VMEM((side, dim, share), low)] * 2
+        + [pltpu.VMEM((groups, side, dim, sub), low)] * 2
         + [pltpu.VMEM((cores, dim, share), low)]
-        + [pltpu.VMEM((cores, side, dim, share), low)] * 2
+        + [pltpu.VMEM((groups, cores, side, dim, sub), low)] * 2
         + [
             dma((5, count)), dma((5, count)),
-            dma((side + 1, side)), dma((side + 1, side)),
-            dma((side,)), dma((side,)),
+            dma((pieces, side)), dma((pieces, side)),
+            dma((groups, side)), dma((groups, side)),
             dma((3, count)), dma((3, count)),
-            dma((cores,)), dma((cores,)), dma((cores,)), dma((cores,)), dma((side + 8,)),
+            dma((cores,)), dma((cores,)), dma((groups, cores)), dma((groups, cores)),
+            dma((pieces + 7,)),
         ],
         compiler_params=pltpu.CompilerParams(
             collective_id=0, has_side_effects=True, vmem_limit_bytes=60 * 1024 * 1024

time: 136 us -> 124 us (0.912)
  Pallas kernels: 134 us -> 121 us
    pallas_call x1, Pallas kernels: 131 us -> 118 us  [head_per_device(): pl.pallas_call(functools.partial(fused_kernel, count, side, cores, dim, t...]
where the time goes in v4:
time: 124 us; the launch traced here: 123 us
  Pallas kernels  121 us (98%)
  other arithmetic  1.28 us (1%)
    pallas_call x1, Pallas kernels, head_per_device(): pl.pallas_call(functools.partial(fused_kernel, count, side, cores, dim, t...  118 us
    pallas_call x1, Pallas kernels, head_per_device(): pl.pallas_call(leave_kernel, out_shape=[jax.ShapeDtypeStruct((rows, width...  3.04 us

profile of v4, /device:TPU:15, one launch (start us, length us, event | category | flops | bytes accessed | tf_op | source)
XLA Modules:
  0.0 123.3 jit_solution(15054501443321794390)
XLA Ops:
  0.6 1.3 %select_reduce_fusion.sources = s32[32]{0:T(128)} fusion(s32[32]{0:T(128)} %bitcast.16), kind=kLoop, calls=%fused_computation | loop fusion | flops 3040 | bytes 256 | tf_op jit(solution)/shard_map/reduce_sum | solution.py:556
  1.9 118.4 %shard_map.111 = (bf16[128,2048]{1,0:T(8,128)(2,1)}, bf16[128,2048]{1,0:T(8,128)(2,1)}, bf16[128,2048]{1,0:T(8,128)(2,1)}, bf16[128,2048]{1,0:T(8,128)(2,1)}) custom-call(s32[32]{0:T(128)} %select_reduce_fusion.sources, s32[32]{0:T(128)} %bitcast.17, bf16[2,64,2048]{2,1,0:T(8,128)(2,1)} %bitcast.10, bf16[2,64,2048]{2,1,0:T(8,128)(2,1)} %bitcast.11, ...), custom_call_target="tpu_custom_call" | custom-call | tf_op jit(solution)/shard_map/pallas_call | solution.py:570
  120.3 3.0 %shard_map.112 = (bf16[128,2048]{1,0:T(8,128)(2,1)}, bf16[128,2048]{1,0:T(8,128)(2,1)}, bf16[128,2048]{1,0:T(8,128)(2,1)}, f32[128,2048]{1,0:T(8,128)}) custom-call(bf16[128,2048]{1,0:T(8,128)(2,1)} %get-tuple-element.12.q_in, bf16[128,2048]{1,0:T(8,128)(2,1)} %get-tuple-element.13.k_in, bf16[128,2048]{1,0:T(8,128)(2,1)} %get-tuple-element.14.v_in, ...), custom_call_target="tpu_custom_call" | custom-call | tf_op jit(solution)/shard_map/pallas_call | solution.py:612
